TPU v7x, 32 devices: a whole 2x2x4 slice. The times are simulated.
32 devices in a mesh: dp: 16 (over z, y, core), tensor: 2 (over x).
Axes of the slice: x: 2, y: 2, z: 4, core: 2. Of those that a mesh axis runs over, the one named last changes fastest.
Arguments:
- layer_input: bfloat16 [16384, 1024], P(('dp', 'tensor')), may hold values from -6 to 6
- segments: int32 [16384], P('dp'), may hold values from 0 to 127, never falling along the last dimension, each value on 1 to 256 neighbouring positions
- w_qkv: bfloat16 [1024, 3, 1024], P(None, None, 'tensor'), may hold values from -0.1875 to 0.1875
- w_out: bfloat16 [1024, 1024], P('tensor'), may hold values from -2 to 2
- w_up: bfloat16 [1024, 4096], P(None, 'tensor'), may hold values from -0.1875 to 0.1875
- w_down: bfloat16 [4096, 1024], P('tensor'), may hold values from -0.09375 to 0.09375
- norm1_gain: float32 [1024], replicated, may hold values from 0.5 to 1.5
- norm1_bias: float32 [1024], replicated, may hold values from -3 to 3
- norm2_gain: float32 [1024], replicated, may hold values from 0.5 to 1.5
- norm2_bias: float32 [1024], replicated, may hold values from -3 to 3
- out_grad: bfloat16 [16384, 1024], P(('dp', 'tensor')), may hold values from -6 to 6
Outputs:
- output: bfloat16 [16384, 1024], P(('dp', 'tensor'))
- input_grad: bfloat16 [16384, 1024], P(('dp', 'tensor'))
- grad_qkv: float32 [1024, 3, 1024], P(None, None, 'tensor')
- grad_out: float32 [1024, 1024], P('tensor')
- grad_up: float32 [1024, 4096], P(None, 'tensor')
- grad_down: float32 [4096, 1024], P('tensor')
- grad_gain1: float32 [1024], replicated
- grad_bias1: float32 [1024], replicated
- grad_gain2: float32 [1024], replicated
- grad_bias2: float32 [1024], replicated
Inputs may be any that keep to these rules, and one draw needn't show every extreme that they name: `segments`: segment ids never fall along the tokens; each protein has 1 to 256 tokens and attends only within its packed row of 512.
All inputs are finite; a program needn't handle non-finite values.
Results may differ from a plain program's by a relative error of at most 0.02.
Values may be sent and summed in bfloat16 or wider, within the bound.
A program may use at most 192 MiB of HBM per device.

v0:
```python
import jax
import jax.numpy as jnp
from jax import lax
from jax.sharding import PartitionSpec as P

HEAD_DIM = 64
ROW_LEN = 512


EPS = 1e-12
NEG_LARGE = -1e30
SQRT_HALF = 0.7071067811865476
INV_ROOT_TWO_PI = 0.3989422804014327


def gelu_exact(values):
    return 0.5 * values * (1.0 + lax.erf(values * SQRT_HALF))


def gelu_slope(values):
    return (
        0.5 * (1.0 + lax.erf(values * SQRT_HALF))
        + values * jnp.exp(-0.5 * values * values) * INV_ROOT_TWO_PI
    )


def layer_norm(values, gain, bias):
    average = jnp.mean(values, axis=-1, keepdims=True)
    centred = values - average
    inverse = lax.rsqrt(jnp.mean(centred * centred, axis=-1, keepdims=True) + EPS)
    normed = centred * inverse
    return (normed * gain + bias, normed, inverse)


def norm_back(grad, normed, inverse, gain):
    scaled = grad * gain
    return inverse * (
        scaled
        - jnp.mean(scaled, axis=-1, keepdims=True)
        - normed * jnp.mean(scaled * normed, axis=-1, keepdims=True)
    )


def masked_scores(queries, keys, row_segments, factor):
    scores = jnp.einsum("qhd,khd->hqk", queries, keys, preferred_element_type=jnp.float32) * factor
    same = row_segments[:, None] == row_segments[None, :]
    return jnp.where(same[None], scores, NEG_LARGE)


def contract_rows(left, right):
    return lax.dot_general(
        left, right, (((0,), (0,)), ((), ())), preferred_element_type=jnp.float32
    )


def contract_cols(left, right):
    return lax.dot_general(
        left, right, (((1,), (1,)), ((), ())), preferred_element_type=jnp.float32
    )


def body(
    layer_input,
    segments,
    w_qkv,
    w_out,
    w_up,
    w_down,
    norm1_gain,
    norm1_bias,
    norm2_gain,
    norm2_bias,
    out_grad,
):
    head_width = HEAD_DIM
    row_length = ROW_LEN
    factor = head_width ** (-0.5)
    qkv_use, out_use = (w_qkv, w_out)
    source = lax.all_gather(layer_input, "tensor", axis=0, tiled=True)
    local_width = qkv_use.shape[2]
    local_heads = local_width // head_width
    group_rows = source.shape[0]
    blocks = group_rows // row_length
    joined = jnp.einsum("td,dsc->tsc", source, qkv_use, preferred_element_type=jnp.float32).astype(
        jnp.bfloat16
    )
    joined_blocks = joined.reshape(blocks, row_length, 3, local_heads, head_width)
    segment_blocks = segments.reshape(blocks, row_length)

    def attend(pack):
        block, row_segments = pack
        scores = masked_scores(block[:, 0], block[:, 1], row_segments, factor)
        top = jnp.max(scores, axis=-1, keepdims=True)
        expo = jnp.exp(scores - top)
        total = jnp.sum(expo, axis=-1, keepdims=True)
        probs = (expo / total).astype(jnp.bfloat16)
        mixed = jnp.einsum("hqk,khd->qhd", probs, block[:, 2], preferred_element_type=jnp.float32)
        return (
            mixed.reshape(row_length, local_width).astype(jnp.bfloat16),
            (top + jnp.log(total))[..., 0],
        )

    attended, log_totals = lax.map(attend, (joined_blocks, segment_blocks))
    attended = attended.reshape(group_rows, local_width)
    attn_out = lax.psum_scatter(
        jnp.dot(attended, out_use, preferred_element_type=jnp.float32).astype(jnp.bfloat16),
        "tensor",
        scatter_dimension=0,
        tiled=True,
    ).astype(jnp.float32)
    hidden, normed_one, inverse_one = layer_norm(
        layer_input.astype(jnp.float32) + attn_out, norm1_gain, norm1_bias
    )
    hidden_low = hidden.astype(jnp.bfloat16)
    hidden_group = lax.all_gather(hidden_low, "tensor", axis=0, tiled=True)
    upper = jnp.dot(hidden_group, w_up, preferred_element_type=jnp.float32)
    active = gelu_exact(upper).astype(jnp.bfloat16)
    ffn_out = lax.psum_scatter(
        jnp.dot(active, w_down, preferred_element_type=jnp.float32).astype(jnp.bfloat16),
        "tensor",
        scatter_dimension=0,
        tiled=True,
    ).astype(jnp.float32)
    result, normed_two, inverse_two = layer_norm(hidden + ffn_out, norm2_gain, norm2_bias)
    grad_result = out_grad.astype(jnp.float32)
    grad_gain2 = jnp.sum(grad_result * normed_two, axis=0)
    grad_bias2 = jnp.sum(grad_result, axis=0)
    grad_second = norm_back(grad_result, normed_two, inverse_two, norm2_gain)
    branch_low = grad_second.astype(jnp.bfloat16)
    branch_group = lax.all_gather(branch_low, "tensor", axis=0, tiled=True)
    grad_active = contract_cols(branch_group, w_down)
    grad_upper = (grad_active * gelu_slope(upper)).astype(jnp.bfloat16)
    grad_down = contract_rows(active, branch_group)
    grad_up = contract_rows(hidden_group, grad_upper)
    hidden_part = lax.psum_scatter(
        contract_cols(grad_upper, w_up).astype(jnp.bfloat16),
        "tensor",
        scatter_dimension=0,
        tiled=True,
    ).astype(jnp.float32)
    grad_hidden = grad_second + hidden_part
    grad_gain1 = jnp.sum(grad_hidden * normed_one, axis=0)
    grad_bias1 = jnp.sum(grad_hidden, axis=0)
    grad_first = norm_back(grad_hidden, normed_one, inverse_one, norm1_gain)
    attn_low = grad_first.astype(jnp.bfloat16)
    attn_group = lax.all_gather(attn_low, "tensor", axis=0, tiled=True)
    grad_mixed = contract_cols(attn_group, out_use).astype(jnp.bfloat16)
    grad_out_w = contract_rows(attended, attn_group)
    grad_mixed_blocks = grad_mixed.reshape(blocks, row_length, local_heads, head_width)

    def attend_back(pack):
        block, row_segments, log_total, grad_block = pack
        queries = block[:, 0]
        keys = block[:, 1]
        values = block[:, 2]
        scores = masked_scores(queries, keys, row_segments, factor)
        probs = jnp.exp(scores - log_total[..., None])
        grad_probs = jnp.einsum(
            "qhd,khd->hqk", grad_block, values, preferred_element_type=jnp.float32
        )
        grad_scores = probs * (grad_probs - jnp.sum(probs * grad_probs, axis=-1, keepdims=True))
        grad_scores = grad_scores.astype(jnp.bfloat16)
        grad_query = (
            jnp.einsum("hqk,khd->qhd", grad_scores, keys, preferred_element_type=jnp.float32)
            * factor
        )
        grad_key = (
            jnp.einsum("hqk,qhd->khd", grad_scores, queries, preferred_element_type=jnp.float32)
            * factor
        )
        grad_value = jnp.einsum(
            "hqk,qhd->khd",
            probs.astype(jnp.bfloat16),
            grad_block,
            preferred_element_type=jnp.float32,
        )
        stacked = jnp.stack([grad_query, grad_key, grad_value], axis=1)
        return stacked.reshape(row_length, 3, local_width).astype(jnp.bfloat16)

    grad_joined = lax.map(
        attend_back, (joined_blocks, segment_blocks, log_totals, grad_mixed_blocks)
    )
    grad_joined = grad_joined.reshape(group_rows, 3, local_width)
    grad_qkv_w = jnp.einsum("td,tsc->dsc", source, grad_joined, preferred_element_type=jnp.float32)
    input_part = lax.psum_scatter(
        jnp.einsum("tsc,dsc->td", grad_joined, qkv_use, preferred_element_type=jnp.float32).astype(
            jnp.bfloat16
        ),
        "tensor",
        scatter_dimension=0,
        tiled=True,
    ).astype(jnp.float32)
    grad_input = grad_first + input_part
    summed_qkv, summed_out, summed_up, summed_down = (
        lax.psum(grad_qkv_w.astype(jnp.bfloat16), "dp").astype(jnp.float32),
        lax.psum(grad_out_w.astype(jnp.bfloat16), "dp").astype(jnp.float32),
        lax.psum(grad_up.astype(jnp.bfloat16), "dp").astype(jnp.float32),
        lax.psum(grad_down.astype(jnp.bfloat16), "dp").astype(jnp.float32),
    )
    summed_gain1, summed_bias1, summed_gain2, summed_bias2 = lax.psum(
        (grad_gain1, grad_bias1, grad_gain2, grad_bias2), ("dp", "tensor")
    )
    return (
        result.astype(jnp.bfloat16),
        grad_input.astype(jnp.bfloat16),
        summed_qkv,
        summed_out,
        summed_up,
        summed_down,
        summed_gain1,
        summed_bias1,
        summed_gain2,
        summed_bias2,
    )


def solution(mesh):
    return jax.shard_map(
        body,
        mesh=mesh,
        in_specs=(
            P(("dp", "tensor"), None),
            P("dp"),
            P(None, None, "tensor"),
            P("tensor", None),
            P(None, "tensor"),
            P("tensor", None),
            P(),
            P(),
            P(),
            P(),
            P(("dp", "tensor"), None),
        ),
        out_specs=(
            P(("dp", "tensor"), None),
            P(("dp", "tensor"), None),
            P(None, None, "tensor"),
            P("tensor", None),
            P(None, "tensor"),
            P("tensor", None),
            P(),
            P(),
            P(),
            P(),
        ),
        check_vma=False,
    )
```

profile of v0, /device:TPU:0, one launch (start us, length us, event | category | flops | bytes accessed | tf_op | source)
XLA Modules:
  0.0 702.7 jit_solution(4263438143487047636)
XLA Ops:
  8.8 36.6 %all-gather.5.cloned.1.call-done = bf16[1024,1024]{1,0:T(8,128)(2,1)} async-done(((bf16[512,1024]{1,0:T(8,128)(2,1)}), bf16[1024,1024]{1,0:T(8,128)(2,1)}) %all-gather.5.cloned.1.call-update) | async-done | bytes 2097168 | tf_op jit(solution)/shard_map/all_gather | solution.py:79
  45.4 6.3 convolution_convert_fusion.2
  51.7 8.9 %reshape.242 = bf16[2,512,3,8,64]{4,3,1,0,2:T(8,128)(2,1)} reshape(bf16[1024,3,512]{2,0,1:T(8,128)(2,1)} %convolution_convert_fusion.2) | data formatting | bytes 6291456 | tf_op jit(solution)/shard_map/reshape | solution.py:87
  60.6 7.6 %copy.35 = bf16[2,512,3,8,64]{1,4,3,2,0:T(8,128)(2,1)} copy(bf16[2,512,3,8,64]{4,3,1,0,2:T(8,128)(2,1)} %reshape.242) | data formatting | bytes 6291456 | tf_op jit(solution)/shard_map/while | solution.py:103
  68.2 24.3 %while.22 = (s32[]{:T(128)}, bf16[2,512,512]{2,1,0:T(8,128)(2,1)}, f32[2,8,512]{2,1,0:T(8,128)S(1)}, bf16[2,512,3,8,64]{1,4,3,2,0:T(8,128)(2,1)}, s32[2,512]{1,0:T(2,128)S(1)}, /*index=5*/s32[]{:T(128)}) while((s32[]{:T(128)}, bf16[2,512,512]{2,1,0:T(8,128)(2,1)}, f32[2,8,512]{2,1,0:T(8,128)S(1)}, bf16[2,512,3,8,64]{1,4,3,2,0:T(8,128)(2,1)}, ...), condition=%wide.region_3.4_spmd, body=%wide.region_0.3_spmd.sunk | while | flops 562556928 | bytes 33692240 | solution.py:103
  73.2 3.2 fusion.87
  85.4 3.2 fusion.87
  92.5 4.1 convolution_convert_fusion.5
  96.7 32.0 %reduce-scatter.5.cloned.1.call-done = bf16[512,1024]{1,0:T(8,128)(2,1)} async-done(((bf16[1024,1024]{1,0:T(8,128)(2,1)}), bf16[512,1024]{1,0:T(8,128)(2,1)}) %reduce-scatter.5.cloned.1.call-update) | async-done | bytes 1048592 | tf_op jit(solution)/shard_map/reduce_scatter | solution.py:105
  134.9 32.7 %all-gather.7.cloned.1.call-done = bf16[1024,1024]{1,0:T(8,128)(2,1)} async-done(((bf16[512,1024]{1,0:T(8,128)(2,1)}), bf16[1024,1024]{1,0:T(8,128)(2,1)}) %all-gather.7.cloned.1.call-update) | async-done | bytes 2097168 | tf_op jit(solution)/shard_map/all_gather | solution.py:115
  167.6 9.5 %multiply_convert_fusion.1 = (bf16[1024,2048]{1,0:T(8,128)(2,1)S(1)}, f32[1024,2048]{1,0:T(8,128)}) fusion(bf16[1024,1024]{1,0:T(8,128)(2,1)} %all-gather.7.cloned.1.call-done, bf16[1024,2048]{1,0:T(8,128)(2,1)} %param.19), kind=kOutput, calls=%fused_computation.55 | convolution fusion | flops 4305453056 | bytes 18874368 | tf_op jit(solution)/shard_map/dot_general | solution.py:116
  179.1 5.6 convolution_convert_fusion.4
  184.8 32.0 %reduce-scatter.7.cloned.1.call-done = bf16[512,1024]{1,0:T(8,128)(2,1)} async-done(((bf16[1024,1024]{1,0:T(8,128)(2,1)}), bf16[512,1024]{1,0:T(8,128)(2,1)}) %reduce-scatter.7.cloned.1.call-update) | async-done | bytes 1048592 | tf_op jit(solution)/shard_map/reduce_scatter | solution.py:118
  216.8 2.8 fusion.49
  221.6 2.9 fusion.47
  224.7 33.0 %all-gather.9.cloned.1.call-done = bf16[1024,1024]{1,0:T(8,128)(2,1)} async-done(((bf16[512,1024]{1,0:T(8,128)(2,1)}), bf16[1024,1024]{1,0:T(8,128)(2,1)}) %all-gather.9.cloned.1.call-update) | async-done | bytes 2097168 | tf_op jit(solution)/shard_map/all_gather | solution.py:130
  257.7 10.3 %fusion.31 = bf16[1024,2048]{1,0:T(8,128)(2,1)S(1)} fusion(f32[1024,2048]{1,0:T(8,128)} %get-tuple-element.165, bf16[1024,1024]{1,0:T(8,128)(2,1)} %all-gather.9.cloned.1.call-done, bf16[2048,1024]{1,0:T(8,128)(2,1)} %param.20), kind=kOutput, calls=%fused_computation.54 | convolution fusion | flops 4315938816 | bytes 18874368 | tf_op jit(solution)/shard_map/dot_general | solution.py:57
  270.0 5.7 convolution_convert_fusion.3
  275.8 32.0 %reduce-scatter.9.cloned.1.call-done = bf16[512,1024]{1,0:T(8,128)(2,1)} async-done(((bf16[1024,1024]{1,0:T(8,128)(2,1)}), bf16[512,1024]{1,0:T(8,128)(2,1)}) %reduce-scatter.9.cloned.1.call-update) | async-done | bytes 1048592 | tf_op jit(solution)/shard_map/reduce_scatter | solution.py:135
  307.8 4.4 multiply_reduce_fusion.1
  312.3 2.5 fusion.46
  314.9 33.2 %all-gather.11.cloned.1.call-done = bf16[1024,1024]{1,0:T(8,128)(2,1)} async-done(((bf16[512,1024]{1,0:T(8,128)(2,1)}), bf16[1024,1024]{1,0:T(8,128)(2,1)}) %all-gather.11.cloned.1.call-update) | async-done | bytes 2097168 | tf_op jit(solution)/shard_map/all_gather | solution.py:146
  348.1 4.1 convolution_convert_fusion.7
  352.2 4.1 reshape.241
  356.3 3.3 copy.39
  359.6 39.4 %while.23 = (s32[]{:T(128)}, bf16[2,512,3,512]{3,1,0,2:T(8,128)(2,1)}, bf16[2,512,3,8,64]{1,4,3,2,0:T(8,128)(2,1)}, s32[2,512]{1,0:T(2,128)S(1)}, f32[2,8,512]{2...) while((s32[]{:T(128)}, bf16[2,512,3,512]{3,1,0,2:T(8,128)(2,1)}, ...), condition=%wide.region_17.18_spmd, body=%wide.region_15.17_spmd.sunk | while | flops 1376776192 | bytes 86104704 | solution.py:180
  362.7 2.9 multiply_reduce_fusion.7
  365.6 2.7 multiply_convert_fusion.3
  370.5 2.3 fusion.93
  374.1 2.6 copy.59
  376.7 2.7 constant_dynamic-update-slice_fusion.5
  382.5 2.9 multiply_reduce_fusion.7
  385.4 2.7 multiply_convert_fusion.3
  390.2 2.3 fusion.93
  393.8 2.6 copy.59
  396.4 2.7 constant_dynamic-update-slice_fusion.5
  399.1 6.6 bitcast_convert_fusion
  406.0 9.6 %convolution_convert_fusion = bf16[2048,1024]{1,0:T(8,128)(2,1)} fusion(bf16[1024,2048]{1,0:T(8,128)(2,1)} %copy-done.27, bf16[1024,1024]{1,0:T(8,128)(2,1)} %all-gather.9.cloned.1.call-done), kind=kOutput, calls=%fused_computation.58 | convolution fusion | flops 4297064448 | bytes 10485760 | tf_op jit(solution)/shard_map/dot_general | solution.py:51
  415.6 6.2 convolution_convert_fusion.1
  421.8 2.3 convolution_convert_fusion.6
  424.1 4.9 convert_bitcast_fusion
  429.7 40.8 %all-reduce = (f32[1024]{0:T(1024)}, f32[1024]{0:T(1024)}, f32[1024]{0:T(1024)}, f32[1024]{0:T(1024)}) all-reduce(f32[1024]{0:T(1024)S(1)} %copy-done.17, f32[1024]{0:T(1024)S(1)} %copy-done.18, f32[1024]{0:T(1024)S(1)} %copy-done.14, f32[1024]{0:T(1024)S(1)} %copy-done.15), channel_id=1, replica_groups=mesh['dp'=16,'tensor'=2] {'dp','tensor'}, use_global_device_ids=true, to_apply=%region_24.25 | all-reduce | flops 4096 | bytes 32768 | tf_op jit(solution)/shard_map/psum | solution.py:200
  470.5 3.2 add_convert_fusion
  473.8 202.5 %all-reduce.4.cloned.1.call-done = (bf16[1024,3,512]{0,2,1:T(8,128)(2,1)}, bf16[512,1024]{1,0:T(8,128)(2,1)}, bf16[1024,2048]{1,0:T(8,128)(2,1)}, bf16[2048,1024]{1,0:T(8,128)(2,1)}) async-done(((bf16[1024,3,512]{0,2,1:T(8,128)(2,1)}, bf16[512,1024]{1,0:T(8,128)(2,1)}, bf16[1024,2048]{1,0:T(8,128)(2,1)}, bf16[2048,1024]{1,0:T(8,128)(2,1)}), (bf16[1024,3,512]{0,2,1:T(8,128)(2,1)}, ...) | async-done | bytes 12582928 | tf_op jit(solution)/shard_map/psum | solution.py:195
  676.2 6.8 convert_element_type.142
  683.0 4.4 convert_element_type.144
  687.5 5.4 copy.42
  692.8 2.8 convert_element_type.140
  (125 shorter events, 46.1 us)
Async XLA Ops:
  7.2 38.2 %copy-start = (bf16[1024,3,512]{2,0,1:T(8,128)(2,1)S(1)}, bf16[1024,3,512]{2,0,1:T(8,128)(2,1)}, u32[]{:S(2)}) copy-start(bf16[1024,3,512]{2,0,1:T(8,128)(2,1)} %param.17) | copy-start | bytes 9437188
  7.2 38.2 %all-gather.5.cloned.1.call-start = ((), (), s32[]{:S(2)}) async-start(), calls=%async_computation.4 | async-start | bytes 3145728 | tf_op jit(solution)/shard_map/all_gather | solution.py:79
  7.9 120.8 %reduce-scatter.5.cloned.1.call-start = ((), (), s32[]{:S(2)}) async-start(), calls=%async_computation.5 | async-start | bytes 3145728 | tf_op jit(solution)/shard_map/reduce_scatter | solution.py:105
  96.6 36.2 %copy-start.12 = (f32[1024]{0:T(1024)S(1)}, f32[1024]{0:T(1024)}, u32[]{:S(2)}) copy-start(f32[1024]{0:T(1024)} %param.21) | copy-start | bytes 12292
  96.6 36.2 %copy-start.16 = (f32[1024]{0:T(1024)S(1)}, f32[1024]{0:T(1024)}, u32[]{:S(2)}) copy-start(f32[1024]{0:T(1024)} %param.22) | copy-start | bytes 12292
  96.6 71.0 %all-gather.7.cloned.1.call-start = ((), (), s32[]{:S(2)}) async-start(), calls=%async_computation.6 | async-start | bytes 3145728 | tf_op jit(solution)/shard_map/all_gather | solution.py:115
  128.7 4.1 copy-start.1
  128.7 4.1 copy-start.3
  134.4 82.5 %reduce-scatter.7.cloned.1.call-start = ((), (), s32[]{:S(2)}) async-start(), calls=%async_computation.7 | async-start | bytes 3145728 | tf_op jit(solution)/shard_map/reduce_scatter | solution.py:118
  167.6 11.5 %copy-start.20 = (bf16[2048,1024]{1,0:T(8,128)(2,1)S(1)}, bf16[2048,1024]{1,0:T(8,128)(2,1)}, u32[]{:S(2)}) copy-start(bf16[2048,1024]{1,0:T(8,128)(2,1)} %param.20) | copy-start | bytes 12582916
  177.1 2.0 copy-start.27
  184.8 35.2 %copy-start.13 = (f32[1024]{0:T(1024)S(1)}, f32[1024]{0:T(1024)}, u32[]{:S(2)}) copy-start(f32[1024]{0:T(1024)} %param.23) | copy-start | bytes 12292
  184.8 72.9 %all-gather.9.cloned.1.call-start = ((), (), s32[]{:S(2)}) async-start(), calls=%async_computation.8 | async-start | bytes 3145728 | tf_op jit(solution)/shard_map/all_gather | solution.py:130
  216.8 3.2 copy-start.8
  219.6 2.0 copy-start.19
  224.5 83.4 %reduce-scatter.9.cloned.1.call-start = ((), (), s32[]{:S(2)}) async-start(), calls=%async_computation.9 | async-start | bytes 3145728 | tf_op jit(solution)/shard_map/reduce_scatter | solution.py:135
  257.7 12.3 %copy-start.21 = (bf16[1024,2048]{1,0:T(8,128)(2,1)S(1)}, bf16[1024,2048]{1,0:T(8,128)(2,1)}, u32[]{:S(2)}) copy-start(bf16[1024,2048]{1,0:T(8,128)(2,1)} %param.19) | copy-start | bytes 12582916
  268.0 2.0 copy-start.25
  275.8 72.3 %all-gather.11.cloned.1.call-start = ((), (), s32[]{:S(2)}) async-start(), calls=%async_computation.10 | async-start | bytes 3145728 | tf_op jit(solution)/shard_map/all_gather | solution.py:146
  307.8 4.4 copy-start.2
  307.8 4.4 copy-start.4
  307.8 4.4 copy-start.5
  307.8 4.4 copy-start.9
  314.9 155.7 %reduce-scatter.11.cloned.1.call-start = ((), (), s32[]{:S(2)}) async-start(), calls=%async_computation.11 | async-start | bytes 3145728 | tf_op jit(solution)/shard_map/reduce_scatter | solution.py:185
  361.1 1.6 copy-start.6
  380.9 1.6 copy-start.6
  405.7 270.6 %all-reduce.4.cloned.1.call-start = ((), (), s32[]{:S(2)}) async-start(), calls=%async_computation.12 | async-start | bytes 25165824 | tf_op jit(solution)/shard_map/psum | solution.py:195
  406.0 9.6 %copy-start.24 = (bf16[1024,1024]{1,0:T(8,128)(2,1)S(1)}, bf16[1024,1024]{1,0:T(8,128)(2,1)}, u32[]{:S(2)}) copy-start(bf16[1024,1024]{1,0:T(8,128)(2,1)} %all-gather.7.cloned.1.call-done) | copy-start | bytes 6291460
  406.0 9.6 %copy-start.26 = (bf16[1024,2048]{1,0:T(8,128)(2,1)S(1)}, bf16[1024,2048]{1,0:T(8,128)(2,1)}, u32[]{:S(2)}) copy-start(bf16[1024,2048]{1,0:T(8,128)(2,1)} %copy-done.25) | copy-start | bytes 12582916
  415.6 6.3 copy-start.10
  415.6 6.3 copy-start.11
  415.6 8.5 %copy-start.23 = (bf16[1024,1024]{1,0:T(8,128)(2,1)S(1)}, bf16[1024,1024]{1,0:T(8,128)(2,1)}, u32[]{:S(2)}) copy-start(bf16[1024,1024]{1,0:T(8,128)(2,1)} %all-gather.5.cloned.1.call-done) | copy-start | bytes 6291460
  421.8 2.3 copy-start.22
  429.0 0.7 copy-start.14
  429.0 0.7 copy-start.15
  429.0 0.7 copy-start.17
  429.0 0.7 copy-start.18
  676.2 6.8 copy-start.7
Sparse Core Ops, SparseCore 0:
  9.5 35.8 all-gather.4
  96.8 31.8 reduce-scatter.4
  134.5 33.0 all-gather.6
  184.9 31.8 reduce-scatter.6
  224.6 33.0 all-gather.8
  275.9 31.8 reduce-scatter.8
  315.0 33.0 all-gather.10
  405.8 31.8 reduce-scatter.10
  442.9 233.3 all-reduce.3
where the time goes:
time: 711 us; the launch traced here: 703 us
  waiting for transfers between devices  435 us (61%)
  matrix products  102 us (14%)
  local copies, waits for them, and re-layouts  59.3 us (8%)
  other arithmetic  49.7 us (7%)
  blocking collectives  40.8 us (6%)
  between operations  14.6 us (2%)
    psum x1, waiting for transfers between devices, body(): lax.psum(grad_qkv_w.astype(jnp.bfloat16), 'dp').astype(jnp.float32)  202 us
    psum x1, blocking collectives, body(): lax.psum((grad_gain1, grad_bias1, grad_gain2, grad_bias2), ('dp', 'tensor'))  40.8 us
    all_gather x1, waiting for transfers between devices, body(): source = lax.all_gather(layer_input, 'tensor', axis=0, tiled=True)  36.6 us
    all_gather x1, waiting for transfers between devices, body(): attn_group = lax.all_gather(attn_low, 'tensor', axis=0, tiled=True)  33.2 us
    all_gather x1, waiting for transfers between devices, body(): branch_group = lax.all_gather(branch_low, 'tensor', axis=0, tiled=True)  33 us
    all_gather x1, waiting for transfers between devices, body(): hidden_group = lax.all_gather(hidden_low, 'tensor', axis=0, tiled=True)  32.7 us
    reduce_scatter x1, waiting for transfers between devices, body(): lax.psum_scatter(jnp.dot(attended, out_use, preferred_element_type=jnp.fl...  32 us
    reduce_scatter x1, waiting for transfers between devices, body(): lax.psum_scatter(contract_cols(grad_upper, w_up).astype(jnp.bfloat16), 't...  32 us
  transfers between devices with their start and end apart: 9, of which 8 were waited for; matrix products, arithmetic and copies ran while one was open for 4% of the time, Pallas kernels for 0%

commit v1 on v0

--- a/solution.py
+++ b/solution.py
@@ -57,6 +57,27 @@
     return lax.dot_general(
         left, right, (((1,), (1,)), ((), ())), preferred_element_type=jnp.float32
     )
+
+
+def _pair_swap(values):
+    return lax.ppermute(values, "tensor", [(0, 1), (1, 0)])
+
+
+def gather_group(values, pair):
+    if pair:
+        return jnp.concatenate([values, _pair_swap(values)], axis=0)
+    return lax.all_gather(values, "tensor", axis=0, tiled=True)
+
+
+def scatter_group(values, pair):
+    if pair:
+        rows = values.shape[0] // 2
+        own = values[:rows].astype(jnp.float32)
+        other = _pair_swap(values[rows:].astype(jnp.bfloat16))
+        return own + other.astype(jnp.float32)
+    return lax.psum_scatter(
+        values.astype(jnp.bfloat16), "tensor", scatter_dimension=0, tiled=True
+    ).astype(jnp.float32)
 
 
 def body(
@@ -76,7 +97,8 @@
     row_length = ROW_LEN
     factor = head_width ** (-0.5)
     qkv_use, out_use = (w_qkv, w_out)
-    source = lax.all_gather(layer_input, "tensor", axis=0, tiled=True)
+    pair = lax.axis_size("tensor") == 2
+    source = gather_group(layer_input, pair)
     local_width = qkv_use.shape[2]
     local_heads = local_width // head_width
     group_rows = source.shape[0]
@@ -85,6 +107,11 @@
         jnp.bfloat16
     )
     joined_blocks = joined.reshape(blocks, row_length, 3, local_heads, head_width)
+    if pair:
+        me = lax.axis_index("tensor")
+        own_seg = lax.dynamic_slice_in_dim(segments, me * row_length, row_length)
+        other_seg = lax.dynamic_slice_in_dim(segments, (1 - me) * row_length, row_length)
+        segments = jnp.concatenate([own_seg, other_seg])
     segment_blocks = segments.reshape(blocks, row_length)
 
     def attend(pack):
@@ -102,48 +129,38 @@
 
     attended, log_totals = lax.map(attend, (joined_blocks, segment_blocks))
     attended = attended.reshape(group_rows, local_width)
-    attn_out = lax.psum_scatter(
-        jnp.dot(attended, out_use, preferred_element_type=jnp.float32).astype(jnp.bfloat16),
-        "tensor",
-        scatter_dimension=0,
-        tiled=True,
-    ).astype(jnp.float32)
+    attn_out = scatter_group(jnp.dot(attended, out_use, preferred_element_type=jnp.float32), pair)
     hidden, normed_one, inverse_one = layer_norm(
         layer_input.astype(jnp.float32) + attn_out, norm1_gain, norm1_bias
     )
     hidden_low = hidden.astype(jnp.bfloat16)
-    hidden_group = lax.all_gather(hidden_low, "tensor", axis=0, tiled=True)
+    hidden_group = gather_group(hidden_low, pair)
     upper = jnp.dot(hidden_group, w_up, preferred_element_type=jnp.float32)
     active = gelu_exact(upper).astype(jnp.bfloat16)
-    ffn_out = lax.psum_scatter(
-        jnp.dot(active, w_down, preferred_element_type=jnp.float32).astype(jnp.bfloat16),
-        "tensor",
-        scatter_dimension=0,
-        tiled=True,
-    ).astype(jnp.float32)
+    ffn_out = scatter_group(jnp.dot(active, w_down, preferred_element_type=jnp.float32), pair)
     result, normed_two, inverse_two = layer_norm(hidden + ffn_out, norm2_gain, norm2_bias)
     grad_result = out_grad.astype(jnp.float32)
     grad_gain2 = jnp.sum(grad_result * normed_two, axis=0)
     grad_bias2 = jnp.sum(grad_result, axis=0)
     grad_second = norm_back(grad_result, normed_two, inverse_two, norm2_gain)
     branch_low = grad_second.astype(jnp.bfloat16)
-    branch_group = lax.all_gather(branch_low, "tensor", axis=0, tiled=True)
+    branch_group = gather_group(branch_low, pair)
     grad_active = contract_cols(branch_group, w_down)
     grad_upper = (grad_active * gelu_slope(upper)).astype(jnp.bfloat16)
     grad_down = contract_rows(active, branch_group)
     grad_up = contract_rows(hidden_group, grad_upper)
-    hidden_part = lax.psum_scatter(
-        contract_cols(grad_upper, w_up).astype(jnp.bfloat16),
-        "tensor",
-        scatter_dimension=0,
-        tiled=True,
-    ).astype(jnp.float32)
+    summed_up, summed_down = lax.psum((grad_up.astype(jnp.bfloat16), grad_down.astype(jnp.bfloat16)), "dp")
+    summed_up, summed_down = summed_up.astype(jnp.float32), summed_down.astype(jnp.float32)
+    hidden_part = scatter_group(contract_cols(grad_upper, w_up), pair)
     grad_hidden = grad_second + hidden_part
     grad_gain1 = jnp.sum(grad_hidden * normed_one, axis=0)
     grad_bias1 = jnp.sum(grad_hidden, axis=0)
     grad_first = norm_back(grad_hidden, normed_one, inverse_one, norm1_gain)
     attn_low = grad_first.astype(jnp.bfloat16)
-    attn_group = lax.all_gather(attn_low, "tensor", axis=0, tiled=True)
+    norm_parts = jnp.zeros((16, grad_gain1.shape[0]), jnp.float32)
+    norm_parts = norm_parts.at[:4].set(jnp.stack([grad_gain1, grad_bias1, grad_gain2, grad_bias2]))
+    norm_sums = lax.psum(norm_parts, ("dp", "tensor"))
+    attn_group = gather_group(attn_low, pair)
     grad_mixed = contract_cols(attn_group, out_use).astype(jnp.bfloat16)
     grad_out_w = contract_rows(attended, attn_group)
     grad_mixed_blocks = grad_mixed.reshape(blocks, row_length, local_heads, head_width)
@@ -182,23 +199,18 @@
     )
     grad_joined = grad_joined.reshape(group_rows, 3, local_width)
     grad_qkv_w = jnp.einsum("td,tsc->dsc", source, grad_joined, preferred_element_type=jnp.float32)
-    input_part = lax.psum_scatter(
-        jnp.einsum("tsc,dsc->td", grad_joined, qkv_use, preferred_element_type=jnp.float32).astype(
-            jnp.bfloat16
-        ),
-        "tensor",
-        scatter_dimension=0,
-        tiled=True,
-    ).astype(jnp.float32)
+    input_part = scatter_group(
+        jnp.einsum("tsc,dsc->td", grad_joined, qkv_use, preferred_element_type=jnp.float32), pair
+    )
     grad_input = grad_first + input_part
-    summed_qkv, summed_out, summed_up, summed_down = (
-        lax.psum(grad_qkv_w.astype(jnp.bfloat16), "dp").astype(jnp.float32),
-        lax.psum(grad_out_w.astype(jnp.bfloat16), "dp").astype(jnp.float32),
-        lax.psum(grad_up.astype(jnp.bfloat16), "dp").astype(jnp.float32),
-        lax.psum(grad_down.astype(jnp.bfloat16), "dp").astype(jnp.float32),
-    )
-    summed_gain1, summed_bias1, summed_gain2, summed_bias2 = lax.psum(
-        (grad_gain1, grad_bias1, grad_gain2, grad_bias2), ("dp", "tensor")
+    late = (grad_qkv_w.astype(jnp.bfloat16), grad_out_w.astype(jnp.bfloat16))
+    late, summed_up, summed_down, norm_sums = lax.optimization_barrier(
+        (late, summed_up, summed_down, norm_sums)
+    )
+    summed_qkv, summed_out = lax.psum(late, "dp")
+    summed_qkv, summed_out = summed_qkv.astype(jnp.float32), summed_out.astype(jnp.float32)
+    summed_gain1, summed_bias1, summed_gain2, summed_bias2 = (
+        norm_sums[0], norm_sums[1], norm_sums[2], norm_sums[3]
     )
     return (
         result.astype(jnp.bfloat16),

time: 711 us -> 663 us (0.932)
  blocking collectives: 40.8 us -> 0 us
  waiting for transfers between devices: 435 us -> 408 us
  local copies, waits for them, and re-layouts: 59.3 us -> 70.6 us
  starting transfers between devices: 1.32 us -> 11 us
    ppermute x0 -> x8, waiting for transfers between devices: none -> 167 us  [_pair_swap(): return lax.ppermute(values, 'tensor', [(0, 1), (1, 0)])]
    all_gather x4 -> x0, waiting for transfers between devices: 135 us -> none  [the longest x1 36.6 us: body(): source = lax.all_gather(layer_input, 'tensor', axis=0, tiled=True)]
    reduce_scatter x4 -> x0, waiting for transfers between devices: 96 us -> none  [the longest x1 32 us: body(): lax.psum_scatter(jnp.dot(attended, out_use, preferred_element_type=jnp.fl...]
    psum x1 -> x0, blocking collectives: 40.8 us -> none  [body(): lax.psum((grad_gain1, grad_bias1, grad_gain2, grad_bias2), ('dp', 'tensor'))]
    psum x1 -> x3, waiting for transfers between devices: 202 us -> 241 us  [the longest x1 114 us: body(): norm_sums = lax.psum(norm_parts, ('dp', 'tensor'))]
    ppermute x0 -> x8, starting transfers between devices: none -> 10.8 us  [_pair_swap(): return lax.ppermute(values, 'tensor', [(0, 1), (1, 0)])]
    unnamed x55 -> x62, local copies, waits for them, and re-layouts: 10.2 us -> 16.4 us
    convert_element_type x3 -> x4, other arithmetic: 14 us -> 17.8 us  [the longest x1 6.8 us: body(): summed_up.astype(jnp.float32)]
  transfers between devices with their start and end apart: 9 -> 11, of which waited for: 8 -> 11; matrix products, arithmetic and copies ran while one was open for 4% -> 17% of each run, Pallas kernels for 0% -> 0%
where the time goes in v1:
time: 663 us; the launch traced here: 654 us
  waiting for transfers between devices  408 us (62%)
  matrix products  101 us (15%)
  local copies, waits for them, and re-layouts  70.6 us (11%)
  other arithmetic  48.7 us (7%)
  between operations  14.5 us (2%)
  starting transfers between devices  11 us (2%)
    ppermute x8, waiting for transfers between devices, _pair_swap(): return lax.ppermute(values, 'tensor', [(0, 1), (1, 0)])  167 us
    psum x1, waiting for transfers between devices, body(): norm_sums = lax.psum(norm_parts, ('dp', 'tensor'))  114 us
    psum x1, waiting for transfers between devices, body(): summed_qkv, summed_out = lax.psum(late, 'dp')  73.6 us
    psum x1, waiting for transfers between devices, body(): lax.psum((grad_up.astype(jnp.bfloat16), grad_down.astype(jnp.bfloat16)),...  53.5 us
    dot_general x3, matrix products, contract_cols(): lax.dot_general(left, right, (((1,), (1,)), ((), ())), preferred_element_...  20.7 us
    dot_general x3, matrix products, contract_rows(): lax.dot_general(left, right, (((0,), (0,)), ((), ())), preferred_element_...  18.6 us
    unnamed x62, local copies, waits for them, and re-layouts  16.4 us
  transfers between devices with their start and end apart: 11, of which 11 were waited for; matrix products, arithmetic and copies ran while one was open for 17% of the time, Pallas kernels for 0%

profile of v1, /device:TPU:0, one launch (start us, length us, event | category | flops | bytes accessed | tf_op | source)
XLA Modules:
  0.0 653.6 jit_solution(17162631048297319724)
XLA Ops:
  7.2 3.0 collective-permute-start
  11.1 22.6 %collective-permute-done = bf16[512,1024]{1,0:T(8,128)(2,1)} collective-permute-done((bf16[512,1024]{1,0:T(8,128)(2,1)}, bf16[512,1024]{1,0:T(8,128)(2,1)}, u32[]{:S(2)}, u32[]{:S(2)}) %collective-permute-start) | collective-permute-done | bytes 1048608 | tf_op jit(solution)/shard_map/ppermute | solution.py:63
  33.8 6.3 convolution_convert_fusion.3
  40.0 8.9 %reshape.269 = bf16[2,512,3,8,64]{4,3,1,0,2:T(8,128)(2,1)} reshape(bf16[1024,3,512]{2,0,1:T(8,128)(2,1)} %convolution_convert_fusion.3) | data formatting | bytes 6291456 | tf_op jit(solution)/shard_map/reshape | solution.py:109
  48.9 7.6 %copy.45 = bf16[2,512,3,8,64]{1,4,3,2,0:T(8,128)(2,1)} copy(bf16[2,512,3,8,64]{4,3,1,0,2:T(8,128)(2,1)} %reshape.269) | data formatting | bytes 6291456 | tf_op jit(solution)/shard_map/while | solution.py:130
  56.5 24.3 %while.23 = (s32[]{:T(128)}, bf16[2,512,512]{2,1,0:T(8,128)(2,1)}, f32[2,8,512]{2,1,0:T(8,128)S(1)}, bf16[2,512,3,8,64]{1,4,3,2,0:T(8,128)(2,1)}, s32[2,512]{1,0:T(2,128)S(1)}, /*index=5*/s32[]{:T(128)}) while((s32[]{:T(128)}, bf16[2,512,512]{2,1,0:T(8,128)(2,1)}, f32[2,8,512]{2,1,0:T(8,128)S(1)}, bf16[2,512,3,8,64]{1,4,3,2,0:T(8,128)(2,1)}, ...), condition=%wide.region_3.4_spmd, body=%wide.region_0.3_spmd.sunk | while | flops 562556928 | bytes 33691740 | solution.py:130
  61.5 3.2 fusion.97
  73.6 3.2 fusion.97
  80.8 2.9 fusion.63
  90.8 20.6 %collective-permute-done.1 = bf16[512,1024]{0,1:T(8,128)(2,1)} collective-permute-done((bf16[512,1024]{0,1:T(8,128)(2,1)}, bf16[512,1024]{0,1:T(8,128)(2,1)}, u32[]{:S(2)}, u32[]{:S(2)}) %collective-permute-start.1) | collective-permute-done | bytes 1048608 | tf_op jit(solution)/shard_map/ppermute | solution.py:63
  111.4 2.7 fusion.59
  117.3 22.0 %collective-permute-done.2 = bf16[512,1024]{0,1:T(8,128)(2,1)S(1)} collective-permute-done((bf16[512,1024]{0,1:T(8,128)(2,1)S(1)}, bf16[512,1024]{0,1:T(8,128)(2,1)S(1)}, u32[]{:S(2)}, u32[]{:S(2)}) %collective-permute-start.2) | collective-permute-done | bytes 1048608 | tf_op jit(solution)/shard_map/ppermute | solution.py:63
  139.4 7.7 %multiply_convert_fusion.1 = (bf16[1024,2048]{1,0:T(8,128)(2,1)S(1)}, f32[1024,2048]{1,0:T(8,128)}) fusion(bf16[1024,2048]{1,0:T(8,128)(2,1)S(1)} %copy-done.22, bf16[512,1024]{0,1:T(8,128)(2,1)S(1)} %collective-permute-done.2, bf16[512,1024]{0,1:T(8,128)(2,1)S(1)} %fusion.44), kind=kOutput, calls=%fused_computation.55 | convolution fusion | flops 4309647360 | bytes 18874368 | tf_op jit(solution)/shard_map/dot_general | solution.py:138
  147.1 4.6 fusion.64
  158.2 19.5 %collective-permute-done.3 = bf16[512,1024]{0,1:T(8,128)(2,1)} collective-permute-done((bf16[512,1024]{0,1:T(8,128)(2,1)}, bf16[512,1024]{0,1:T(8,128)(2,1)}, u32[]{:S(2)}, u32[]{:S(2)}) %collective-permute-start.3) | collective-permute-done | bytes 1048608 | tf_op jit(solution)/shard_map/ppermute | solution.py:63
  177.7 3.1 fusion.57
  183.8 20.9 %collective-permute-done.4 = bf16[512,1024]{0,1:T(8,128)(2,1)S(1)} collective-permute-done((bf16[512,1024]{0,1:T(8,128)(2,1)S(1)}, bf16[512,1024]{0,1:T(8,128)(2,1)S(1)}, u32[]{:S(2)}, u32[]{:S(2)}) %collective-permute-start.4) | collective-permute-done | bytes 1048608 | tf_op jit(solution)/shard_map/ppermute | solution.py:63
  204.7 6.3 convolution_convert_fusion
  211.0 8.7 %fusion.31 = bf16[1024,2048]{1,0:T(8,128)(2,1)} fusion(f32[1024,2048]{1,0:T(8,128)S(1)} %bitcast.157, bf16[2048,1024]{1,0:T(8,128)(2,1)S(1)} %copy-done.21, bf16[512,1024]{0,1:T(8,128)(2,1)S(1)} %collective-permute-done.4, bf16[512,1024]{0,1:T(8,128)(2,1)S(1)} %fusion.46), kind=kOutput, calls=%fused_computation.54 | convolution fusion | flops 4320133120 | bytes 18874368 | tf_op jit(solution)/shard_map/dot_general | solution.py:57
  219.7 8.3 %convolution_convert_fusion.1 = bf16[1024,2048]{1,0:T(8,128)(2,1)} fusion(bf16[1024,2048]{1,0:T(8,128)(2,1)} %fusion.31, bf16[512,1024]{0,1:T(8,128)(2,1)S(1)} %copy-done.24, bf16[512,1024]{0,1:T(8,128)(2,1)S(1)} %copy-done.15), kind=kOutput, calls=%fused_computation.58 | convolution fusion | flops 4301258752 | bytes 10485760 | tf_op jit(solution)/shard_map/dot_general | solution.py:51
  228.2 7.7 %fusion.65 = f32[1024,1024]{0,1:T(8,128)S(1)} fusion(bf16[1024,2048]{1,0:T(8,128)(2,1)} %fusion.31, bf16[1024,2048]{1,0:T(8,128)(2,1)} %param.21), kind=kOutput, calls=%fused_computation.132 | convolution fusion | flops 4294967296 | bytes 12582912 | tf_op jit(solution)/shard_map/dot_general | solution.py:57
  236.7 20.3 %collective-permute-done.5 = bf16[512,1024]{0,1:T(8,128)(2,1)S(1)} collective-permute-done((bf16[512,1024]{0,1:T(8,128)(2,1)S(1)}, bf16[512,1024]{0,1:T(8,128)(2,1)S(1)}, u32[]{:S(2)}, u32[]{:S(2)}) %collective-permute-start.5) | collective-permute-done | bytes 1048608 | tf_op jit(solution)/shard_map/ppermute | solution.py:63
  257.1 2.9 multiply_reduce_fusion.1
  262.7 19.5 %collective-permute-done.6 = bf16[512,1024]{0,1:T(8,128)(2,1)} collective-permute-done((bf16[512,1024]{0,1:T(8,128)(2,1)}, bf16[512,1024]{0,1:T(8,128)(2,1)}, u32[]{:S(2)}, u32[]{:S(2)}) %collective-permute-start.6) | collective-permute-done | bytes 1048608 | tf_op jit(solution)/shard_map/ppermute | solution.py:63
  282.1 4.2 convolution_convert_fusion.5
  286.3 4.1 reshape.268
  290.4 3.3 copy.54
  293.7 39.7 %while.24 = (s32[]{:T(128)}, bf16[2,512,3,512]{3,1,0,2:T(8,128)(2,1)}, bf16[2,512,3,8,64]{1,4,3,2,0:T(8,128)(2,1)}, s32[2,512]{1,0:T(2,128)S(1)}, f32[2,8,512]{2...) while((s32[]{:T(128)}, bf16[2,512,3,512]{3,1,0,2:T(8,128)(2,1)}, ...), condition=%wide.region_14.15_spmd, body=%wide.region_12.14_spmd.sunk | while | flops 1376776192 | bytes 86104192 | solution.py:197
  299.1 2.9 multiply_reduce_fusion.7
  302.0 2.7 multiply_convert_fusion.3
  308.2 2.6 copy.83
  310.7 2.7 constant_dynamic-update-slice_fusion.5
  318.8 2.9 multiply_reduce_fusion.7
  321.7 2.7 multiply_convert_fusion.3
  327.9 2.6 copy.83
  330.4 2.7 constant_dynamic-update-slice_fusion.5
  333.4 7.8 %convolution_convert_fusion.2 = bf16[1024,3,512]{2,0,1:T(8,128)(2,1)} fusion(bf16[1024,3,512]{2,0,1:T(8,128)(2,1)} %bitcast.152, bf16[512,1024]{1,0:T(8,128)(2,1)} %collective-permute-done, bf16[512,1024]{1,0:T(8,128)(2,1)} %param.17), kind=kOutput, calls=%fused_computation.65 | convolution fusion | flops 3226992640 | bytes 8388608 | tf_op jit(solution)/shard_map/td,tsc->dsc/dot_general | solution.py:201
  341.2 4.0 convolution_convert_fusion.4
  345.2 53.5 %all-reduce.11.cloned.1.call-done = (bf16[1024,2048]{1,0:T(8,128)(2,1)}, bf16[2048,1024]{1,0:T(8,128)(2,1)}) async-done(((bf16[1024,2048]{1,0:T(8,128)(2,1)}, bf16[2048,1024]{1,0:T(8,128)(2,1)}), (bf16[1024,2048]{1,0:T(8,128)(2,1)}, bf16[2048,1024]{1,0:T(8,128)(2,1)})) %all-reduce.11.cloned.1.call-update) | async-done | bytes 8388624 | tf_op jit(solution)/shard_map/psum | solution.py:152
  398.8 6.8 %convert_element_type.124 = f32[1024,2048]{1,0:T(8,128)} convert(bf16[1024,2048]{1,0:T(8,128)(2,1)} %get-tuple-element.169) | non-fusion elementwise | flops 2097152 | bytes 12582912 | tf_op jit(solution)/shard_map/convert_element_type | solution.py:153
  405.6 4.4 convert_element_type.126
  410.0 113.6 %all-reduce.7.cloned.1.call-done = f32[16,1024]{1,0:T(8,128)} async-done(((f32[16,1024]{1,0:T(8,128)}), f32[16,1024]{1,0:T(8,128)}) %all-reduce.7.cloned.1.call-update) | async-done | bytes 65552 | tf_op jit(solution)/shard_map/psum | solution.py:162
  523.6 5.3 convolution_bitcast_fusion
  535.9 21.7 %collective-permute-done.7 = bf16[512,1024]{0,1:T(8,128)(2,1)} collective-permute-done((bf16[512,1024]{0,1:T(8,128)(2,1)}, bf16[512,1024]{0,1:T(8,128)(2,1)}, u32[]{:S(2)}, u32[]{:S(2)}) %collective-permute-start.7) | collective-permute-done | bytes 1048608 | tf_op jit(solution)/shard_map/ppermute | solution.py:63
  557.7 5.1 fusion.40
  566.6 73.6 %all-reduce.9.cloned.1.call-done = (bf16[1024,3,512]{2,0,1:T(8,128)(2,1)}, bf16[512,1024]{1,0:T(8,128)(2,1)}) async-done(((bf16[1024,3,512]{2,0,1:T(8,128)(2,1)}, bf16[512,1024]{1,0:T(8,128)(2,1)}), (bf16[1024,3,512]{2,0,1:T(8,128)(2,1)}, bf16[512,1024]{1,0:T(8,128)(2,1)})) %all-reduce.9.cloned.1.call-update) | async-done | bytes 4194320 | tf_op jit(solution)/shard_map/psum | solution.py:210
  640.1 2.9 convert_element_type.128
  643.1 3.6 convert_element_type.127
  (139 shorter events, 70.6 us)
Async XLA Ops:
  7.2 26.6 %copy-start = (bf16[1024,3,512]{2,0,1:T(8,128)(2,1)S(1)}, bf16[1024,3,512]{2,0,1:T(8,128)(2,1)}, u32[]{:S(2)}) copy-start(bf16[1024,3,512]{2,0,1:T(8,128)(2,1)} %param.19) | copy-start | bytes 9437188
  7.2 391.6 %all-reduce.11.cloned.1.call-start = ((), (), s32[]{:S(2)}) async-start(), calls=%async_computation.2 | async-start | bytes 16777216 | tf_op jit(solution)/shard_map/psum | solution.py:152
  7.2 26.5 %collective-permute-start = (bf16[512,1024]{1,0:T(8,128)(2,1)}, bf16[512,1024]{1,0:T(8,128)(2,1)}, u32[]{:S(2)}, u32[]{:S(2)}) collective-permute-start(bf16[512,1024]{1,0:T(8,128)(2,1)} %param.17), channel_id=1, source_target_pairs={{0,1},{1,0},{2,3},{3,2},{4,5},{5,4},{6,7},{7,6},{8,9},{9,8},{10,11... | collective-permute-start | bytes 3145736 | tf_op jit(solution)/shard_map/ppermute | solution.py:63
  83.6 2.0 copy-start.13
  86.8 24.6 %collective-permute-start.1 = (bf16[512,1024]{0,1:T(8,128)(2,1)}, bf16[512,1024]{0,1:T(8,128)(2,1)}, u32[]{:S(2)}, u32[]{:S(2)}) collective-permute-start(bf16[512,1024]{0,1:T(8,128)(2,1)} %slice.135), channel_id=1, source_target_pairs={{0,1},{1,0},{2,3},{3,2},{4,5},{5,4},{6,7},{7,6},{8,9},{9,8},{10,11... | collective-permute-start | bytes 3145736 | tf_op jit(solution)/shard_map/ppermute | solution.py:63
  90.8 24.6 %copy-start.16 = (f32[1024]{0:T(1024)S(1)}, f32[1024]{0:T(1024)}, u32[]{:S(2)}) copy-start(f32[1024]{0:T(1024)} %param.23) | copy-start | bytes 12292
  90.8 24.6 %copy-start.18 = (f32[1024]{0:T(1024)S(1)}, f32[1024]{0:T(1024)}, u32[]{:S(2)}) copy-start(f32[1024]{0:T(1024)} %param.24) | copy-start | bytes 12292
  114.1 1.3 copy-start.1
  114.1 25.3 %copy-start.22 = (bf16[1024,2048]{1,0:T(8,128)(2,1)S(1)}, bf16[1024,2048]{1,0:T(8,128)(2,1)}, u32[]{:S(2)}) copy-start(bf16[1024,2048]{1,0:T(8,128)(2,1)} %param.21) | copy-start | bytes 12582916
  115.8 31.3 %copy-start.14 = (bf16[512,1024]{0,1:T(8,128)(2,1)}, bf16[512,1024]{0,1:T(8,128)(2,1)S(1)}, u32[]{:S(2)}) copy-start(bf16[512,1024]{0,1:T(8,128)(2,1)S(1)} %fusion.44) | copy-start | bytes 3145732
  115.8 31.3 %copy-start.20 = (bf16[2048,1024]{1,0:T(8,128)(2,1)S(1)}, bf16[2048,1024]{1,0:T(8,128)(2,1)}, u32[]{:S(2)}) copy-start(bf16[2048,1024]{1,0:T(8,128)(2,1)} %param.22) | copy-start | bytes 12582916
  115.8 23.5 %collective-permute-start.2 = (bf16[512,1024]{0,1:T(8,128)(2,1)S(1)}, bf16[512,1024]{0,1:T(8,128)(2,1)S(1)}, u32[]{:S(2)}, u32[]{:S(2)}) collective-permute-start(bf16[512,1024]{0,1:T(8,128)(2,1)S(1)} %fusion.44), channel_id=1, source_target_pairs={{0,1},{1,0},{2,3},{3,2},{4,5},{5,4},{6,7},{7,6},{8,9},{9,8},{10,11... | collective-permute-start | bytes 3145736 | tf_op jit(solution)/shard_map/ppermute | solution.py:63
  139.4 7.7 %copy-start.23 = (bf16[512,1024]{0,1:T(8,128)(2,1)}, bf16[512,1024]{0,1:T(8,128)(2,1)S(1)}, u32[]{:S(2)}) copy-start(bf16[512,1024]{0,1:T(8,128)(2,1)S(1)} %collective-permute-done.2) | copy-start | bytes 3145732
  147.1 4.6 copy-start.26
  151.7 2.0 copy-start.12
  154.8 22.9 %collective-permute-start.3 = (bf16[512,1024]{0,1:T(8,128)(2,1)}, bf16[512,1024]{0,1:T(8,128)(2,1)}, u32[]{:S(2)}, u32[]{:S(2)}) collective-permute-start(bf16[512,1024]{0,1:T(8,128)(2,1)} %slice.134), channel_id=1, source_target_pairs={{0,1},{1,0},{2,3},{3,2},{4,5},{5,4},{6,7},{7,6},{8,9},{9,8},{10,11... | collective-permute-start | bytes 3145736 | tf_op jit(solution)/shard_map/ppermute | solution.py:63
  158.2 22.9 %copy-start.6 = (bf16[512,1024]{0,1:T(8,128)(2,1)S(1)}, bf16[512,1024]{0,1:T(8,128)(2,1)}, u32[]{:S(2)}) copy-start(bf16[512,1024]{0,1:T(8,128)(2,1)} %copy.49) | copy-start | bytes 3145732
  158.2 22.9 %copy-start.17 = (f32[1024]{0:T(1024)S(1)}, f32[1024]{0:T(1024)}, u32[]{:S(2)}) copy-start(f32[1024]{0:T(1024)} %param.25) | copy-start | bytes 12292
  180.9 2.0 copy-start.3
  181.2 23.5 %copy-start.27 = (bf16[1024,2048]{1,0:T(8,128)(2,1)S(1)}, bf16[1024,2048]{1,0:T(8,128)(2,1)}, u32[]{:S(2)}) copy-start(bf16[1024,2048]{1,0:T(8,128)(2,1)} %copy-done.26) | copy-start | bytes 12582916
  182.2 28.7 %slice-start = ((s8[8388608]{0:T(1024)(128)(4,1)}), s8[4194304]{0:T(1024)(128)(4,1)S(1)}, s32[]{:S(2)}) async-start(s8[8388608]{0:T(1024)(128)(4,1)} %bitcast.156), calls=%async_computation.3 | async-start | bytes 8388608
  182.8 28.1 %copy-start.21 = (bf16[2048,1024]{1,0:T(8,128)(2,1)S(1)}, bf16[2048,1024]{1,0:T(8,128)(2,1)}, u32[]{:S(2)}) copy-start(bf16[2048,1024]{1,0:T(8,128)(2,1)} %param.22) | copy-start | bytes 12582916
  182.8 28.1 %slice-start.1 = ((s8[8388608]{0:T(1024)(128)(4,1)}), s8[4194304]{0:T(1024)(128)(4,1)S(1)}, s32[]{:S(2)}) async-start(s8[8388608]{0:T(1024)(128)(4,1)} %bitcast.156), calls=%async_computation.4 | async-start | bytes 8388608
  182.9 21.8 %collective-permute-start.4 = (bf16[512,1024]{0,1:T(8,128)(2,1)S(1)}, bf16[512,1024]{0,1:T(8,128)(2,1)S(1)}, u32[]{:S(2)}, u32[]{:S(2)}) collective-permute-start(bf16[512,1024]{0,1:T(8,128)(2,1)S(1)} %fusion.46), channel_id=1, source_target_pairs={{0,1},{1,0},{2,3},{3,2},{4,5},{5,4},{6,7},{7,6},{8,9},{9,8},{10,11... | collective-permute-start | bytes 3145736 | tf_op jit(solution)/shard_map/ppermute | solution.py:63
  211.0 8.8 %copy-start.15 = (bf16[512,1024]{0,1:T(8,128)(2,1)S(1)}, bf16[512,1024]{0,1:T(8,128)(2,1)}, u32[]{:S(2)}) copy-start(bf16[512,1024]{0,1:T(8,128)(2,1)} %copy-done.14) | copy-start | bytes 3145732
  211.0 8.8 %copy-start.24 = (bf16[512,1024]{0,1:T(8,128)(2,1)S(1)}, bf16[512,1024]{0,1:T(8,128)(2,1)}, u32[]{:S(2)}) copy-start(bf16[512,1024]{0,1:T(8,128)(2,1)} %copy-done.23) | copy-start | bytes 3145732
  228.1 29.0 %copy-start.19 = (f32[1024]{0:T(1024)S(1)}, f32[1024]{0:T(1024)}, u32[]{:S(2)}) copy-start(f32[1024]{0:T(1024)} %param.26) | copy-start | bytes 12292
  228.1 295.5 %all-reduce.7.cloned.1.call-start = ((), (), s32[]{:S(2)}) async-start(), calls=%async_computation | async-start | bytes 131072 | tf_op jit(solution)/shard_map/psum | solution.py:162
  228.1 28.9 %copy-start.4 = (f32[512,1024]{0,1:T(8,128)S(1)}, f32[512,1024]{0,1:T(8,128)}, u32[]{:S(2)}) copy-start(f32[512,1024]{0,1:T(8,128)} %copy-done.3) | copy-start | bytes 6291460
  228.1 28.9 %copy-start.7 = (bf16[512,1024]{0,1:T(8,128)(2,1)S(1)}, bf16[512,1024]{0,1:T(8,128)(2,1)}, u32[]{:S(2)}) copy-start(bf16[512,1024]{0,1:T(8,128)(2,1)} %copy.49) | copy-start | bytes 3145732
  235.9 21.2 %copy-start.2 = (f32[512,1024]{0,1:T(8,128)S(1)}, f32[512,1024]{0,1:T(8,128)}, u32[]{:S(2)}) copy-start(f32[512,1024]{0,1:T(8,128)} %copy-done.1) | copy-start | bytes 6291460
  236.1 21.0 %collective-permute-start.5 = (bf16[512,1024]{0,1:T(8,128)(2,1)S(1)}, bf16[512,1024]{0,1:T(8,128)(2,1)S(1)}, u32[]{:S(2)}, u32[]{:S(2)}) collective-permute-start(bf16[512,1024]{0,1:T(8,128)(2,1)S(1)} %slice.133), channel_id=1, source_target_pairs={{0,1},{1,0},{2,3},{3,2},{4,5},{5,4},{6,7},{7,6},{8,9},{9,8},{10,11... | collective-permute-start | bytes 3145736 | tf_op jit(solution)/shard_map/ppermute | solution.py:63
  260.0 1.7 copy-start.5
  261.7 20.5 %collective-permute-start.6 = (bf16[512,1024]{0,1:T(8,128)(2,1)}, bf16[512,1024]{0,1:T(8,128)(2,1)}, u32[]{:S(2)}, u32[]{:S(2)}) collective-permute-start(bf16[512,1024]{0,1:T(8,128)(2,1)} %fusion.55), channel_id=1, source_target_pairs={{0,1},{1,0},{2,3},{3,2},{4,5},{5,4},{6,7},{7,6},{8,9},{9,8},{10,11... | collective-permute-start | bytes 3145736 | tf_op jit(solution)/shard_map/ppermute | solution.py:63
  262.6 377.5 %all-reduce.9.cloned.1.call-start = ((), (), s32[]{:S(2)}) async-start(), calls=%async_computation.1 | async-start | bytes 8388608 | tf_op jit(solution)/shard_map/psum | solution.py:210
  295.5 1.3 copy-start.8
  315.2 1.3 copy-start.8
  333.4 7.8 %copy-start.25 = (bf16[2,512,512]{2,1,0:T(8,128)(2,1)S(1)}, bf16[2,512,512]{2,1,0:T(8,128)(2,1)}, u32[]{:S(2)}) copy-start(bf16[2,512,512]{2,1,0:T(8,128)(2,1)} %get-tuple-element.87) | copy-start | bytes 3145732
  398.8 6.8 %copy-start.9 = (bf16[2048,1024]{1,0:T(8,128)(2,1)S(1)}, bf16[2048,1024]{1,0:T(8,128)(2,1)}, u32[]{:S(2)}) copy-start(bf16[2048,1024]{1,0:T(8,128)(2,1)} %get-tuple-element.170) | copy-start | bytes 12582916
  528.9 2.0 copy-start.11
  532.1 25.6 %collective-permute-start.7 = (bf16[512,1024]{0,1:T(8,128)(2,1)}, bf16[512,1024]{0,1:T(8,128)(2,1)}, u32[]{:S(2)}, u32[]{:S(2)}) collective-permute-start(bf16[512,1024]{0,1:T(8,128)(2,1)} %slice.132), channel_id=1, source_target_pairs={{0,1},{1,0},{2,3},{3,2},{4,5},{5,4},{6,7},{7,6},{8,9},{9,8},{10,11... | collective-permute-start | bytes 3145736 | tf_op jit(solution)/shard_map/ppermute | solution.py:63
  640.1 2.9 copy-start.10
Sparse Core Ops, SparseCore 0:
  228.2 170.5 all-reduce.10
  404.3 119.1 all-reduce.6
  527.4 112.7 all-reduce.8

commit v2 on v1

--- a/solution.py
+++ b/solution.py
@@ -157,9 +157,6 @@
     grad_bias1 = jnp.sum(grad_hidden, axis=0)
     grad_first = norm_back(grad_hidden, normed_one, inverse_one, norm1_gain)
     attn_low = grad_first.astype(jnp.bfloat16)
-    norm_parts = jnp.zeros((16, grad_gain1.shape[0]), jnp.float32)
-    norm_parts = norm_parts.at[:4].set(jnp.stack([grad_gain1, grad_bias1, grad_gain2, grad_bias2]))
-    norm_sums = lax.psum(norm_parts, ("dp", "tensor"))
     attn_group = gather_group(attn_low, pair)
     grad_mixed = contract_cols(attn_group, out_use).astype(jnp.bfloat16)
     grad_out_w = contract_rows(attended, attn_group)
@@ -204,14 +201,13 @@
     )
     grad_input = grad_first + input_part
     late = (grad_qkv_w.astype(jnp.bfloat16), grad_out_w.astype(jnp.bfloat16))
-    late, summed_up, summed_down, norm_sums = lax.optimization_barrier(
-        (late, summed_up, summed_down, norm_sums)
+    norm_parts = (grad_gain1, grad_bias1, grad_gain2, grad_bias2)
+    late, summed_up, summed_down, norm_parts = lax.optimization_barrier(
+        (late, summed_up, summed_down, norm_parts)
     )
     summed_qkv, summed_out = lax.psum(late, "dp")
     summed_qkv, summed_out = summed_qkv.astype(jnp.float32), summed_out.astype(jnp.float32)
-    summed_gain1, summed_bias1, summed_gain2, summed_bias2 = (
-        norm_sums[0], norm_sums[1], norm_sums[2], norm_sums[3]
-    )
+    summed_gain1, summed_bias1, summed_gain2, summed_bias2 = lax.psum(norm_parts, ("dp", "tensor"))
     return (
         result.astype(jnp.bfloat16),
         grad_input.astype(jnp.bfloat16),

time: 663 us -> 581 us (0.88)
  waiting for transfers between devices: 408 us -> 286 us
  blocking collectives: 0 us -> 40.3 us
    psum x1 -> x0, waiting for transfers between devices: 114 us -> none  [body(): norm_sums = lax.psum(norm_parts, ('dp', 'tensor'))]
    psum x1, waiting for transfers between devices: 53.5 us -> 101 us  [body(): lax.psum((grad_up.astype(jnp.bfloat16), grad_down.astype(jnp.bfloat16)),...]
    psum x1, waiting for transfers between devices: 73.6 us -> 30.1 us  [body(): summed_qkv, summed_out = lax.psum(late, 'dp')]
    psum x0 -> x1, blocking collectives: none -> 40.3 us  [body(): lax.psum(norm_parts, ('dp', 'tensor'))]
    ppermute x8, waiting for transfers between devices: 167 us -> 155 us  [_pair_swap(): return lax.ppermute(values, 'tensor', [(0, 1), (1, 0)])]
    unnamed x62 -> x98, local copies, waits for them, and re-layouts: 16.4 us -> 19 us
  transfers between devices with their start and end apart: 11 -> 10, of which waited for: 11 -> 10; matrix products, arithmetic and copies ran while one was open for 17% -> 17% of each run, Pallas kernels for 0% -> 0%
where the time goes in v2:
time: 581 us; the launch traced here: 572 us
  waiting for transfers between devices  286 us (49%)
  matrix products  94.9 us (16%)
  local copies, waits for them, and re-layouts  72.9 us (13%)
  other arithmetic  51.4 us (9%)
  blocking collectives  40.3 us (7%)
  between operations  14.9 us (3%)
  starting transfers between devices  10.9 us (2%)
    ppermute x8, waiting for transfers between devices, _pair_swap(): return lax.ppermute(values, 'tensor', [(0, 1), (1, 0)])  155 us
    psum x1, waiting for transfers between devices, body(): lax.psum((grad_up.astype(jnp.bfloat16), grad_down.astype(jnp.bfloat16)),...  101 us
    psum x1, blocking collectives, body(): lax.psum(norm_parts, ('dp', 'tensor'))  40.3 us
    psum x1, waiting for transfers between devices, body(): summed_qkv, summed_out = lax.psum(late, 'dp')  30.1 us
    unnamed x98, local copies, waits for them, and re-layouts  19 us
    dot_general x3, matrix products, contract_cols(): lax.dot_general(left, right, (((1,), (1,)), ((), ())), preferred_element_...  18.4 us
    dot_general x3, matrix products, contract_rows(): lax.dot_general(left, right, (((0,), (0,)), ((), ())), preferred_element_...  16.6 us
  transfers between devices with their start and end apart: 10, of which 10 were waited for; matrix products, arithmetic and copies ran while one was open for 17% of the time, Pallas kernels for 0%

profile of v2, /device:TPU:0, one launch (start us, length us, event | category | flops | bytes accessed | tf_op | source)
XLA Modules:
  0.0 571.7 jit_solution(7604517351712207048)
XLA Ops:
  7.2 3.0 collective-permute-start
  11.1 22.6 %collective-permute-done = bf16[512,1024]{1,0:T(8,128)(2,1)} collective-permute-done((bf16[512,1024]{1,0:T(8,128)(2,1)}, bf16[512,1024]{1,0:T(8,128)(2,1)}, u32[]{:S(2)}, u32[]{:S(2)}) %collective-permute-start) | collective-permute-done | bytes 1048608 | tf_op jit(solution)/shard_map/ppermute | solution.py:63
  33.7 6.3 %convolution_convert_fusion.3 = bf16[1024,3,512]{2,0,1:T(8,128)(2,1)} fusion(bf16[1024,3,512]{2,0,1:T(8,128)(2,1)S(1)} %copy-done, bf16[512,1024]{1,0:T(8,128)(2,1)} %collective-permute-done, bf16[512,1024]{1,0:T(8,128)(2,1)} %param.15), kind=kOutput, calls=%fused_computation.66 | convolution fusion | flops 3226992640 | bytes 8388608 | tf_op jit(solution)/shard_map/td,dsc->tsc/dot_general | solution.py:106
  40.0 8.9 %reshape.243 = bf16[2,512,3,8,64]{4,3,1,0,2:T(8,128)(2,1)} reshape(bf16[1024,3,512]{2,0,1:T(8,128)(2,1)} %convolution_convert_fusion.3) | data formatting | bytes 6291456 | tf_op jit(solution)/shard_map/reshape | solution.py:109
  48.9 7.6 %copy.45 = bf16[2,512,3,8,64]{1,4,3,2,0:T(8,128)(2,1)} copy(bf16[2,512,3,8,64]{4,3,1,0,2:T(8,128)(2,1)} %reshape.243) | data formatting | bytes 6291456 | tf_op jit(solution)/shard_map/while | solution.py:130
  56.5 24.3 %while.22 = (s32[]{:T(128)}, bf16[2,512,512]{2,1,0:T(8,128)(2,1)}, f32[2,8,512]{2,1,0:T(8,128)S(1)}, bf16[2,512,3,8,64]{1,4,3,2,0:T(8,128)(2,1)}, s32[2,512]{1,0:T(2,128)S(1)}, /*index=5*/s32[]{:T(128)}) while((s32[]{:T(128)}, bf16[2,512,512]{2,1,0:T(8,128)(2,1)}, f32[2,8,512]{2,1,0:T(8,128)S(1)}, bf16[2,512,3,8,64]{1,4,3,2,0:T(8,128)(2,1)}, ...), condition=%wide.region_3.4_spmd, body=%wide.region_0.3_spmd.sunk | while | flops 562556928 | bytes 33691740 | solution.py:130
  61.5 3.2 fusion.96
  73.7 3.2 fusion.96
  80.8 2.9 fusion.62
  90.8 20.6 %collective-permute-done.1 = bf16[512,1024]{0,1:T(8,128)(2,1)} collective-permute-done((bf16[512,1024]{0,1:T(8,128)(2,1)}, bf16[512,1024]{0,1:T(8,128)(2,1)}, u32[]{:S(2)}, u32[]{:S(2)}) %collective-permute-start.1) | collective-permute-done | bytes 1048608 | tf_op jit(solution)/shard_map/ppermute | solution.py:63
  111.4 2.7 fusion.59
  117.4 22.0 %collective-permute-done.2 = bf16[512,1024]{0,1:T(8,128)(2,1)S(1)} collective-permute-done((bf16[512,1024]{0,1:T(8,128)(2,1)S(1)}, bf16[512,1024]{0,1:T(8,128)(2,1)S(1)}, u32[]{:S(2)}, u32[]{:S(2)}) %collective-permute-start.2) | collective-permute-done | bytes 1048608 | tf_op jit(solution)/shard_map/ppermute | solution.py:63
  139.4 7.7 %multiply_convert_fusion.1 = (bf16[1024,2048]{1,0:T(8,128)(2,1)S(1)}, f32[1024,2048]{1,0:T(8,128)}) fusion(bf16[1024,2048]{1,0:T(8,128)(2,1)S(1)} %copy-done.37, bf16[512,1024]{0,1:T(8,128)(2,1)S(1)} %collective-permute-done.2, bf16[512,1024]{0,1:T(8,128)(2,1)S(1)} %fusion.44), kind=kOutput, calls=%fused_computation.55 | convolution fusion | flops 4309647360 | bytes 18874368 | tf_op jit(solution)/shard_map/dot_general | solution.py:138
  147.1 4.6 fusion.63
  158.3 19.5 %collective-permute-done.3 = bf16[512,1024]{0,1:T(8,128)(2,1)} collective-permute-done((bf16[512,1024]{0,1:T(8,128)(2,1)}, bf16[512,1024]{0,1:T(8,128)(2,1)}, u32[]{:S(2)}, u32[]{:S(2)}) %collective-permute-start.3) | collective-permute-done | bytes 1048608 | tf_op jit(solution)/shard_map/ppermute | solution.py:63
  177.8 3.1 fusion.57
  184.4 20.9 %collective-permute-done.4 = bf16[512,1024]{0,1:T(8,128)(2,1)S(1)} collective-permute-done((bf16[512,1024]{0,1:T(8,128)(2,1)S(1)}, bf16[512,1024]{0,1:T(8,128)(2,1)S(1)}, u32[]{:S(2)}, u32[]{:S(2)}) %collective-permute-start.4) | collective-permute-done | bytes 1048608 | tf_op jit(solution)/shard_map/ppermute | solution.py:63
  205.3 9.7 %fusion.31 = bf16[1024,2048]{1,0:T(8,128)(2,1)S(1)} fusion(f32[1024,2048]{1,0:T(8,128)} %get-tuple-element.182, bf16[2048,1024]{1,0:T(8,128)(2,1)S(1)} %copy-done.36, bf16[512,1024]{0,1:T(8,128)(2,1)S(1)} %collective-permute-done.4, bf16[512,1024]{0,1:T(8,128)(2,1)S(1)} %fusion.46), kind=kOutput, calls=%fused_computation.54 | convolution fusion | flops 4320133120 | bytes 18874368 | tf_op jit(solution)/shard_map/dot_general | solution.py:57
  215.1 4.5 fusion.64
  223.4 20.6 %collective-permute-done.5 = bf16[512,1024]{0,1:T(8,128)(2,1)} collective-permute-done((bf16[512,1024]{0,1:T(8,128)(2,1)}, bf16[512,1024]{0,1:T(8,128)(2,1)}, u32[]{:S(2)}, u32[]{:S(2)}) %collective-permute-start.5) | collective-permute-done | bytes 1048608 | tf_op jit(solution)/shard_map/ppermute | solution.py:63
  244.0 5.8 %multiply_reduce_fusion.1 = (f32[1024]{0:T(1024)}, f32[512]{0:T(512)S(1)}, f32[512]{0:T(512)S(1)}, f32[1024]{0:T(1024)}, f32[512,1024]{0,1:T(8,128)S(1)}, /*index=5*/bf16[512,1024]{0,1:T(8,128)(2,1)}) fusion(f32[512,1024]{0,1:T(8,128)} %copy-done.1, f32[512]{0:T(512)S(1)} %add_rsqrt_fusion.1, f32[512]{0:T(512)S(1)} %broadcast_multiply_fusion.5, ...), kind=kLoop, calls=%fused_computation.89 | loop fusion | flops 12055552 | bytes 11571200 | tf_op jit(solution)/shard_map/reduce_sum | solution.py:156
  252.5 6.2 %convolution_convert_fusion = bf16[2048,1024]{1,0:T(8,128)(2,1)} fusion(bf16[1024,2048]{1,0:T(8,128)(2,1)S(1)} %copy-done.45, bf16[512,1024]{0,1:T(8,128)(2,1)S(1)} %copy-done.43, bf16[512,1024]{0,1:T(8,128)(2,1)S(1)} %copy-done.14), kind=kOutput, calls=%fused_computation.57 | convolution fusion | flops 4301258752 | bytes 10485760 | tf_op jit(solution)/shard_map/dot_general | solution.py:51
  258.7 6.0 %convolution_convert_fusion.1 = bf16[1024,2048]{1,0:T(8,128)(2,1)} fusion(bf16[1024,2048]{1,0:T(8,128)(2,1)S(1)} %copy-done.47, bf16[512,1024]{0,1:T(8,128)(2,1)S(1)} %copy-done.41, bf16[512,1024]{0,1:T(8,128)(2,1)S(1)} %copy-done.17), kind=kOutput, calls=%fused_computation.58 | convolution fusion | flops 4301258752 | bytes 10485760 | tf_op jit(solution)/shard_map/dot_general | solution.py:51
  264.8 7.1 %collective-permute-done.6 = bf16[512,1024]{0,1:T(8,128)(2,1)} collective-permute-done((bf16[512,1024]{0,1:T(8,128)(2,1)}, bf16[512,1024]{0,1:T(8,128)(2,1)}, u32[]{:S(2)}, u32[]{:S(2)}) %collective-permute-start.6) | collective-permute-done | bytes 1048608 | tf_op jit(solution)/shard_map/ppermute | solution.py:63
  271.9 4.2 convolution_convert_fusion.5
  276.1 4.1 reshape.242
  280.2 3.3 copy.54
  283.5 39.6 %while.23 = (s32[]{:T(128)}, bf16[2,512,3,512]{3,1,0,2:T(8,128)(2,1)}, bf16[2,512,3,8,64]{1,4,3,2,0:T(8,128)(2,1)}, s32[2,512]{1,0:T(2,128)S(1)}, f32[2,8,512]{2...) while((s32[]{:T(128)}, bf16[2,512,3,512]{3,1,0,2:T(8,128)(2,1)}, ...), condition=%wide.region_14.15_spmd, body=%wide.region_12.14_spmd.sunk | while | flops 1376776192 | bytes 86104192 | solution.py:194
  288.9 2.9 multiply_reduce_fusion.7
  291.8 2.7 multiply_convert_fusion.3
  297.9 2.6 copy.83
  300.6 2.7 constant_dynamic-update-slice_fusion.5
  308.7 2.9 multiply_reduce_fusion.7
  311.6 2.7 multiply_convert_fusion.3
  317.7 2.6 copy.83
  320.3 2.7 constant_dynamic-update-slice_fusion.5
  323.1 4.3 convolution_convert_fusion.4
  327.4 6.5 %convolution_convert_fusion.2 = bf16[1024,3,512]{2,0,1:T(8,128)(2,1)} fusion(bf16[1024,3,512]{2,0,1:T(8,128)(2,1)S(1)} %bitcast.137, bf16[512,1024]{1,0:T(8,128)(2,1)} %collective-permute-done, bf16[512,1024]{1,0:T(8,128)(2,1)S(1)} %copy-done.15), kind=kOutput, calls=%fused_computation.65 | convolution fusion | flops 3226992640 | bytes 8388608 | tf_op jit(solution)/shard_map/td,tsc->dsc/dot_general | solution.py:198
  333.8 101.2 %all-reduce.8.cloned.1.call-done = (bf16[1024,2048]{1,0:T(8,128)(2,1)}, bf16[2048,1024]{1,0:T(8,128)(2,1)}) async-done(((bf16[1024,2048]{1,0:T(8,128)(2,1)}, bf16[2048,1024]{1,0:T(8,128)(2,1)}), (bf16[1024,2048]{1,0:T(8,128)(2,1)}, bf16[2048,1024]{1,0:T(8,128)(2,1)})) %all-reduce.8.cloned.1.call-update) | async-done | bytes 8388624 | tf_op jit(solution)/shard_map/psum | solution.py:152
  435.1 6.8 %convert_element_type.124 = f32[1024,2048]{1,0:T(8,128)} convert(bf16[1024,2048]{1,0:T(8,128)(2,1)} %get-tuple-element.167) | non-fusion elementwise | flops 2097152 | bytes 12582912 | tf_op jit(solution)/shard_map/convert_element_type | solution.py:153
  441.9 4.4 convert_element_type.126
  446.3 5.3 convolution_bitcast_fusion
  458.6 21.4 %collective-permute-done.7 = bf16[512,1024]{0,1:T(8,128)(2,1)} collective-permute-done((bf16[512,1024]{0,1:T(8,128)(2,1)}, bf16[512,1024]{0,1:T(8,128)(2,1)}, u32[]{:S(2)}, u32[]{:S(2)}) %collective-permute-start.7) | collective-permute-done | bytes 1048608 | tf_op jit(solution)/shard_map/ppermute | solution.py:63
  480.1 5.0 fusion.40
  487.4 40.3 %all-reduce = (f32[1024]{0:T(1024)}, f32[1024]{0:T(1024)}, f32[1024]{0:T(1024)}, f32[1024]{0:T(1024)}) all-reduce(f32[1024]{0:T(1024)S(1)} %copy-done.32, f32[1024]{0:T(1024)S(1)} %copy-done.33, f32[1024]{0:T(1024)S(1)} %copy-done.30, f32[1024]{0:T(1024)S(1)} %copy-done.31), channel_id=1, replica_groups=mesh['dp'=16,'tensor'=2] {'dp','tensor'}, use_global_device_ids=true, to_apply=%region_23.24 | all-reduce | flops 4096 | bytes 32768 | tf_op jit(solution)/shard_map/psum | solution.py:210
  527.7 30.1 %all-reduce.6.cloned.1.call-done = (bf16[1024,3,512]{2,0,1:T(8,128)(2,1)}, bf16[512,1024]{1,0:T(8,128)(2,1)}) async-done(((bf16[1024,3,512]{2,0,1:T(8,128)(2,1)}, bf16[512,1024]{1,0:T(8,128)(2,1)}), (bf16[1024,3,512]{2,0,1:T(8,128)(2,1)}, bf16[512,1024]{1,0:T(8,128)(2,1)})) %all-reduce.6.cloned.1.call-update) | async-done | bytes 4194320 | tf_op jit(solution)/shard_map/psum | solution.py:208
  557.9 2.9 convert_element_type.128
  560.8 3.6 convert_element_type.127
  (170 shorter events, 72.5 us)
Async XLA Ops:
  7.2 26.6 %copy-start = (bf16[1024,3,512]{2,0,1:T(8,128)(2,1)S(1)}, bf16[1024,3,512]{2,0,1:T(8,128)(2,1)}, u32[]{:S(2)}) copy-start(bf16[1024,3,512]{2,0,1:T(8,128)(2,1)} %param.17) | copy-start | bytes 9437188
  7.2 427.9 %all-reduce.8.cloned.1.call-start = ((), (), s32[]{:S(2)}) async-start(), calls=%async_computation.1 | async-start | bytes 16777216 | tf_op jit(solution)/shard_map/psum | solution.py:152
  7.2 26.5 %collective-permute-start = (bf16[512,1024]{1,0:T(8,128)(2,1)}, bf16[512,1024]{1,0:T(8,128)(2,1)}, u32[]{:S(2)}, u32[]{:S(2)}) collective-permute-start(bf16[512,1024]{1,0:T(8,128)(2,1)} %param.15), channel_id=1, source_target_pairs={{0,1},{1,0},{2,3},{3,2},{4,5},{5,4},{6,7},{7,6},{8,9},{9,8},{10,11... | collective-permute-start | bytes 3145736 | tf_op jit(solution)/shard_map/ppermute | solution.py:63
  86.8 24.6 %collective-permute-start.1 = (bf16[512,1024]{0,1:T(8,128)(2,1)}, bf16[512,1024]{0,1:T(8,128)(2,1)}, u32[]{:S(2)}, u32[]{:S(2)}) collective-permute-start(bf16[512,1024]{0,1:T(8,128)(2,1)} %slice.103), channel_id=1, source_target_pairs={{0,1},{1,0},{2,3},{3,2},{4,5},{5,4},{6,7},{7,6},{8,9},{9,8},{10,11... | collective-permute-start | bytes 3145736 | tf_op jit(solution)/shard_map/ppermute | solution.py:63
  90.8 24.6 %copy-start.18 = (f32[1024]{0:T(1024)S(1)}, f32[1024]{0:T(1024)}, u32[]{:S(2)}) copy-start(f32[1024]{0:T(1024)} %param.21) | copy-start | bytes 12292
  90.8 24.6 %copy-start.29 = (f32[1024]{0:T(1024)S(1)}, f32[1024]{0:T(1024)}, u32[]{:S(2)}) copy-start(f32[1024]{0:T(1024)} %param.22) | copy-start | bytes 12292
  114.1 25.3 %copy-start.37 = (bf16[1024,2048]{1,0:T(8,128)(2,1)S(1)}, bf16[1024,2048]{1,0:T(8,128)(2,1)}, u32[]{:S(2)}) copy-start(bf16[1024,2048]{1,0:T(8,128)(2,1)} %param.19) | copy-start | bytes 12582916
  114.1 135.7 %copy-start.20 = (f32[512]{0:T(512)}, f32[512]{0:T(512)S(1)}, u32[]{:S(2)}) copy-start(f32[512]{0:T(512)S(1)} %broadcast_multiply_fusion.5) | copy-start | bytes 6148
  115.4 134.4 %copy-start.22 = (f32[512]{0:T(512)}, f32[512]{0:T(512)S(1)}, u32[]{:S(2)}) copy-start(f32[512]{0:T(512)S(1)} %add_rsqrt_fusion.1) | copy-start | bytes 6148
  115.8 31.3 %copy-start.16 = (bf16[512,1024]{0,1:T(8,128)(2,1)}, bf16[512,1024]{0,1:T(8,128)(2,1)S(1)}, u32[]{:S(2)}) copy-start(bf16[512,1024]{0,1:T(8,128)(2,1)S(1)} %fusion.44) | copy-start | bytes 3145732
  115.8 31.3 %copy-start.35 = (bf16[2048,1024]{1,0:T(8,128)(2,1)S(1)}, bf16[2048,1024]{1,0:T(8,128)(2,1)}, u32[]{:S(2)}) copy-start(bf16[2048,1024]{1,0:T(8,128)(2,1)} %param.20) | copy-start | bytes 12582916
  115.8 23.5 %collective-permute-start.2 = (bf16[512,1024]{0,1:T(8,128)(2,1)S(1)}, bf16[512,1024]{0,1:T(8,128)(2,1)S(1)}, u32[]{:S(2)}, u32[]{:S(2)}) collective-permute-start(bf16[512,1024]{0,1:T(8,128)(2,1)S(1)} %fusion.44), channel_id=1, source_target_pairs={{0,1},{1,0},{2,3},{3,2},{4,5},{5,4},{6,7},{7,6},{8,9},{9,8},{10,11... | collective-permute-start | bytes 3145736 | tf_op jit(solution)/shard_map/ppermute | solution.py:63
  139.4 7.7 %copy-start.40 = (bf16[512,1024]{0,1:T(8,128)(2,1)}, bf16[512,1024]{0,1:T(8,128)(2,1)S(1)}, u32[]{:S(2)}) copy-start(bf16[512,1024]{0,1:T(8,128)(2,1)S(1)} %collective-permute-done.2) | copy-start | bytes 3145732
  147.1 4.6 copy-start.44
  154.8 22.9 %collective-permute-start.3 = (bf16[512,1024]{0,1:T(8,128)(2,1)}, bf16[512,1024]{0,1:T(8,128)(2,1)}, u32[]{:S(2)}, u32[]{:S(2)}) collective-permute-start(bf16[512,1024]{0,1:T(8,128)(2,1)} %slice.102), channel_id=1, source_target_pairs={{0,1},{1,0},{2,3},{3,2},{4,5},{5,4},{6,7},{7,6},{8,9},{9,8},{10,11... | collective-permute-start | bytes 3145736 | tf_op jit(solution)/shard_map/ppermute | solution.py:63
  158.3 22.9 %copy-start.5 = (bf16[512,1024]{0,1:T(8,128)(2,1)S(1)}, bf16[512,1024]{0,1:T(8,128)(2,1)}, u32[]{:S(2)}) copy-start(bf16[512,1024]{0,1:T(8,128)(2,1)} %copy.49) | copy-start | bytes 3145732
  158.3 22.9 %copy-start.24 = (f32[1024]{0:T(1024)S(1)}, f32[1024]{0:T(1024)}, u32[]{:S(2)}) copy-start(f32[1024]{0:T(1024)} %param.23) | copy-start | bytes 12292
  180.9 2.5 copy-start.3
  181.2 24.1 %copy-start.36 = (bf16[2048,1024]{1,0:T(8,128)(2,1)S(1)}, bf16[2048,1024]{1,0:T(8,128)(2,1)}, u32[]{:S(2)}) copy-start(bf16[2048,1024]{1,0:T(8,128)(2,1)} %param.20) | copy-start | bytes 12582916
  183.4 31.6 %copy-start.13 = (bf16[512,1024]{0,1:T(8,128)(2,1)}, bf16[512,1024]{0,1:T(8,128)(2,1)S(1)}, u32[]{:S(2)}) copy-start(bf16[512,1024]{0,1:T(8,128)(2,1)S(1)} %fusion.46) | copy-start | bytes 3145732
  183.5 21.8 %collective-permute-start.4 = (bf16[512,1024]{0,1:T(8,128)(2,1)S(1)}, bf16[512,1024]{0,1:T(8,128)(2,1)S(1)}, u32[]{:S(2)}, u32[]{:S(2)}) collective-permute-start(bf16[512,1024]{0,1:T(8,128)(2,1)S(1)} %fusion.46), channel_id=1, source_target_pairs={{0,1},{1,0},{2,3},{3,2},{4,5},{5,4},{6,7},{7,6},{8,9},{9,8},{10,11... | collective-permute-start | bytes 3145736 | tf_op jit(solution)/shard_map/ppermute | solution.py:63
  205.3 9.8 %copy-start.42 = (bf16[512,1024]{0,1:T(8,128)(2,1)}, bf16[512,1024]{0,1:T(8,128)(2,1)S(1)}, u32[]{:S(2)}) copy-start(bf16[512,1024]{0,1:T(8,128)(2,1)S(1)} %collective-permute-done.4) | copy-start | bytes 3145732
  205.3 9.8 %copy-start.38 = (bf16[1024,2048]{1,0:T(8,128)(2,1)S(1)}, bf16[1024,2048]{1,0:T(8,128)(2,1)}, u32[]{:S(2)}) copy-start(bf16[1024,2048]{1,0:T(8,128)(2,1)} %param.19) | copy-start | bytes 12582916
  215.1 4.6 copy-start.46
  215.1 28.9 %copy-start.34 = (f32[1024]{0:T(1024)S(1)}, f32[1024]{0:T(1024)}, u32[]{:S(2)}) copy-start(f32[1024]{0:T(1024)} %param.24) | copy-start | bytes 12292
  222.8 21.2 %collective-permute-start.5 = (bf16[512,1024]{0,1:T(8,128)(2,1)}, bf16[512,1024]{0,1:T(8,128)(2,1)}, u32[]{:S(2)}, u32[]{:S(2)}) collective-permute-start(bf16[512,1024]{0,1:T(8,128)(2,1)} %slice.101), channel_id=1, source_target_pairs={{0,1},{1,0},{2,3},{3,2},{4,5},{5,4},{6,7},{7,6},{8,9},{9,8},{10,11... | collective-permute-start | bytes 3145736 | tf_op jit(solution)/shard_map/ppermute | solution.py:63
  223.4 26.5 %copy-start.2 = (f32[512,1024]{0,1:T(8,128)S(1)}, f32[512,1024]{0,1:T(8,128)}, u32[]{:S(2)}) copy-start(f32[512,1024]{0,1:T(8,128)} %copy-done.1) | copy-start | bytes 6291460
  244.0 7.9 %copy-start.45 = (bf16[1024,2048]{1,0:T(8,128)(2,1)S(1)}, bf16[1024,2048]{1,0:T(8,128)(2,1)}, u32[]{:S(2)}) copy-start(bf16[1024,2048]{1,0:T(8,128)(2,1)} %copy-done.44) | copy-start | bytes 12582916
  249.8 2.7 copy-start.43
  251.5 7.2 %copy-start.17 = (bf16[512,1024]{0,1:T(8,128)(2,1)S(1)}, bf16[512,1024]{0,1:T(8,128)(2,1)}, u32[]{:S(2)}) copy-start(bf16[512,1024]{0,1:T(8,128)(2,1)} %copy-done.16) | copy-start | bytes 3145732
  251.5 7.2 %copy-start.41 = (bf16[512,1024]{0,1:T(8,128)(2,1)S(1)}, bf16[512,1024]{0,1:T(8,128)(2,1)}, u32[]{:S(2)}) copy-start(bf16[512,1024]{0,1:T(8,128)(2,1)} %copy-done.40) | copy-start | bytes 3145732
  251.5 7.2 %copy-start.47 = (bf16[1024,2048]{1,0:T(8,128)(2,1)S(1)}, bf16[1024,2048]{1,0:T(8,128)(2,1)}, u32[]{:S(2)}) copy-start(bf16[1024,2048]{1,0:T(8,128)(2,1)} %copy-done.46) | copy-start | bytes 12582916
  251.5 20.4 %collective-permute-start.6 = (bf16[512,1024]{0,1:T(8,128)(2,1)}, bf16[512,1024]{0,1:T(8,128)(2,1)}, u32[]{:S(2)}, u32[]{:S(2)}) collective-permute-start(bf16[512,1024]{0,1:T(8,128)(2,1)} %fusion.55), channel_id=1, source_target_pairs={{0,1},{1,0},{2,3},{3,2},{4,5},{5,4},{6,7},{7,6},{8,9},{9,8},{10,11... | collective-permute-start | bytes 3145736 | tf_op jit(solution)/shard_map/ppermute | solution.py:63
  264.8 293.1 %all-reduce.6.cloned.1.call-start = ((), (), s32[]{:S(2)}) async-start(), calls=%async_computation | async-start | bytes 8388608 | tf_op jit(solution)/shard_map/psum | solution.py:208
  323.1 4.3 copy-start.15
  323.1 4.3 copy-start.39
  435.1 6.8 %copy-start.7 = (bf16[2048,1024]{1,0:T(8,128)(2,1)S(1)}, bf16[2048,1024]{1,0:T(8,128)(2,1)}, u32[]{:S(2)}) copy-start(bf16[2048,1024]{1,0:T(8,128)(2,1)} %get-tuple-element.168) | copy-start | bytes 12582916
  453.7 26.3 %copy-start.19 = (f32[1024]{0:T(1024)S(1)}, f32[1024]{0:T(1024)}, u32[]{:S(2)}) copy-start(f32[1024]{0:T(1024)} %param.21) | copy-start | bytes 12292
  453.7 26.3 %copy-start.21 = (f32[512]{0:T(512)S(1)}, f32[512]{0:T(512)}, u32[]{:S(2)}) copy-start(f32[512]{0:T(512)} %copy-done.20) | copy-start | bytes 6148
  453.7 26.3 %copy-start.23 = (f32[512]{0:T(512)S(1)}, f32[512]{0:T(512)}, u32[]{:S(2)}) copy-start(f32[512]{0:T(512)} %copy-done.22) | copy-start | bytes 6148
  453.7 26.3 %copy-start.26 = (f32[512]{0:T(512)S(1)}, f32[512]{0:T(512)}, u32[]{:S(2)}) copy-start(f32[512]{0:T(512)} %copy-done.25) | copy-start | bytes 6148
  453.7 26.4 %copy-start.28 = (f32[512]{0:T(512)S(1)}, f32[512]{0:T(512)}, u32[]{:S(2)}) copy-start(f32[512]{0:T(512)} %copy-done.27) | copy-start | bytes 6148
  454.8 25.2 %collective-permute-start.7 = (bf16[512,1024]{0,1:T(8,128)(2,1)}, bf16[512,1024]{0,1:T(8,128)(2,1)}, u32[]{:S(2)}, u32[]{:S(2)}) collective-permute-start(bf16[512,1024]{0,1:T(8,128)(2,1)} %slice.100), channel_id=1, source_target_pairs={{0,1},{1,0},{2,3},{3,2},{4,5},{5,4},{6,7},{7,6},{8,9},{9,8},{10,11... | collective-permute-start | bytes 3145736 | tf_op jit(solution)/shard_map/ppermute | solution.py:63
  458.6 28.8 %copy-start.30 = (f32[1024]{0:T(1024)S(1)}, f32[1024]{0:T(1024)}, u32[]{:S(2)}) copy-start(f32[1024]{0:T(1024)} %get-tuple-element.87) | copy-start | bytes 12292
  458.6 28.8 %copy-start.31 = (f32[1024]{0:T(1024)S(1)}, f32[1024]{0:T(1024)}, u32[]{:S(2)}) copy-start(f32[1024]{0:T(1024)} %get-tuple-element.88) | copy-start | bytes 12292
  458.6 28.8 %copy-start.32 = (f32[1024]{0:T(1024)S(1)}, f32[1024]{0:T(1024)}, u32[]{:S(2)}) copy-start(f32[1024]{0:T(1024)} %get-tuple-element.85) | copy-start | bytes 12292
  458.6 28.8 %copy-start.33 = (f32[1024]{0:T(1024)S(1)}, f32[1024]{0:T(1024)}, u32[]{:S(2)}) copy-start(f32[1024]{0:T(1024)} %get-tuple-element.86) | copy-start | bytes 12292
  557.9 2.9 copy-start.8
  (11 other events, 19.1 us)
Sparse Core Ops, SparseCore 0:
  264.9 170.1 all-reduce.7
  446.5 111.3 all-reduce.5

commit v3 on v2

--- a/solution.py
+++ b/solution.py
@@ -222,9 +222,162 @@
     )
 
 
+def attend_row(qkv, row_segments, factor):
+    rows, _, width = qkv.shape
+    heads = width // HEAD_DIM
+    block = qkv.reshape(rows, 3, heads, HEAD_DIM)
+    scores = masked_scores(block[:, 0], block[:, 1], row_segments, factor)
+    top = jnp.max(scores, axis=-1, keepdims=True)
+    expo = jnp.exp(scores - top)
+    total = jnp.sum(expo, axis=-1, keepdims=True)
+    probs = (expo / total).astype(jnp.bfloat16)
+    mixed = jnp.einsum("hqk,khd->qhd", probs, block[:, 2], preferred_element_type=jnp.float32)
+    return mixed.reshape(rows, width).astype(jnp.bfloat16), (top + jnp.log(total))[..., 0]
+
+
+def attend_row_back(qkv, row_segments, log_total, grad_mixed, factor):
+    rows, _, width = qkv.shape
+    heads = width // HEAD_DIM
+    block = qkv.reshape(rows, 3, heads, HEAD_DIM)
+    queries = block[:, 0]
+    keys = block[:, 1]
+    values = block[:, 2]
+    grad_block = grad_mixed.reshape(rows, heads, HEAD_DIM)
+    scores = masked_scores(queries, keys, row_segments, factor)
+    probs = jnp.exp(scores - log_total[..., None])
+    grad_probs = jnp.einsum("qhd,khd->hqk", grad_block, values, preferred_element_type=jnp.float32)
+    grad_scores = probs * (grad_probs - jnp.sum(probs * grad_probs, axis=-1, keepdims=True))
+    grad_scores = grad_scores.astype(jnp.bfloat16)
+    grad_query = (
+        jnp.einsum("hqk,khd->qhd", grad_scores, keys, preferred_element_type=jnp.float32) * factor
+    )
+    grad_key = (
+        jnp.einsum("hqk,qhd->khd", grad_scores, queries, preferred_element_type=jnp.float32) * factor
+    )
+    grad_value = jnp.einsum(
+        "hqk,qhd->khd", probs.astype(jnp.bfloat16), grad_block, preferred_element_type=jnp.float32
+    )
+    stacked = jnp.stack([grad_query, grad_key, grad_value], axis=1)
+    return stacked.reshape(rows, 3, width).astype(jnp.bfloat16)
+
+
+def body_pair(
+    layer_input,
+    segments,
+    w_qkv,
+    w_out,
+    w_up,
+    w_down,
+    norm1_gain,
+    norm1_bias,
+    norm2_gain,
+    norm2_bias,
+    out_grad,
+):
+    factor = HEAD_DIM ** (-0.5)
+    rows = layer_input.shape[0]
+    me = lax.axis_index("tensor")
+    seg_o = lax.dynamic_slice_in_dim(segments, me * rows, rows)
+    seg_x = lax.dynamic_slice_in_dim(segments, (1 - me) * rows, rows)
+
+    def project(values):
+        return jnp.einsum("td,dsc->tsc", values, w_qkv, preferred_element_type=jnp.float32).astype(
+            jnp.bfloat16
+        )
+
+    in_x = _pair_swap(layer_input)
+    qkv_o = project(layer_input)
+    qkv_x = project(in_x)
+    att_x, lse_x = attend_row(qkv_x, seg_x, factor)
+    part_x = jnp.dot(att_x, w_out, preferred_element_type=jnp.float32)
+    recv = _pair_swap(part_x.astype(jnp.bfloat16))
+    att_o, lse_o = attend_row(qkv_o, seg_o, factor)
+    part_o = jnp.dot(att_o, w_out, preferred_element_type=jnp.float32)
+    attn_out = part_o + recv.astype(jnp.float32)
+    hidden, normed_one, inverse_one = layer_norm(
+        layer_input.astype(jnp.float32) + attn_out, norm1_gain, norm1_bias
+    )
+    hid_o = hidden.astype(jnp.bfloat16)
+
+    hid_x = _pair_swap(hid_o)
+    up_o = jnp.dot(hid_o, w_up, preferred_element_type=jnp.float32)
+    act_o = gelu_exact(up_o).astype(jnp.bfloat16)
+    up_x = jnp.dot(hid_x, w_up, preferred_element_type=jnp.float32)
+    act_x = gelu_exact(up_x).astype(jnp.bfloat16)
+    down_x = jnp.dot(act_x, w_down, preferred_element_type=jnp.float32)
+    recv = _pair_swap(down_x.astype(jnp.bfloat16))
+    down_o = jnp.dot(act_o, w_down, preferred_element_type=jnp.float32)
+    ffn_out = down_o + recv.astype(jnp.float32)
+    result, normed_two, inverse_two = layer_norm(hidden + ffn_out, norm2_gain, norm2_bias)
+
+    grad_result = out_grad.astype(jnp.float32)
+    grad_gain2 = jnp.sum(grad_result * normed_two, axis=0)
+    grad_bias2 = jnp.sum(grad_result, axis=0)
+    grad_second = norm_back(grad_result, normed_two, inverse_two, norm2_gain)
+    br_o = grad_second.astype(jnp.bfloat16)
+
+    br_x = _pair_swap(br_o)
+    gu_o = (contract_cols(br_o, w_down) * gelu_slope(up_o)).astype(jnp.bfloat16)
+    gu_x = (contract_cols(br_x, w_down) * gelu_slope(up_x)).astype(jnp.bfloat16)
+    hp_x = contract_cols(gu_x, w_up)
+    recv = _pair_swap(hp_x.astype(jnp.bfloat16))
+    grad_down = contract_rows(act_o, br_o) + contract_rows(act_x, br_x)
+    grad_up = contract_rows(hid_o, gu_o) + contract_rows(hid_x, gu_x)
+    summed_up, summed_down = lax.psum(
+        (grad_up.astype(jnp.bfloat16), grad_down.astype(jnp.bfloat16)), "dp"
+    )
+    summed_up, summed_down = summed_up.astype(jnp.float32), summed_down.astype(jnp.float32)
+    hp_o = contract_cols(gu_o, w_up)
+    grad_hidden = grad_second + hp_o + recv.astype(jnp.float32)
+
+    grad_gain1 = jnp.sum(grad_hidden * normed_one, axis=0)
+    grad_bias1 = jnp.sum(grad_hidden, axis=0)
+    grad_first = norm_back(grad_hidden, normed_one, inverse_one, norm1_gain)
+    da_o = grad_first.astype(jnp.bfloat16)
+
+    da_x = _pair_swap(da_o)
+    gm_o = contract_cols(da_o, w_out).astype(jnp.bfloat16)
+    gj_o = attend_row_back(qkv_o, seg_o, lse_o, gm_o, factor)
+    gm_x = contract_cols(da_x, w_out).astype(jnp.bfloat16)
+    gj_x = attend_row_back(qkv_x, seg_x, lse_x, gm_x, factor)
+
+    def back_project(values):
+        return jnp.einsum("tsc,dsc->td", values, w_qkv, preferred_element_type=jnp.float32)
+
+    ip_x = back_project(gj_x)
+    recv = _pair_swap(ip_x.astype(jnp.bfloat16))
+    grad_out_w = contract_rows(att_o, da_o) + contract_rows(att_x, da_x)
+    grad_qkv_w = jnp.einsum(
+        "td,tsc->dsc", layer_input, gj_o, preferred_element_type=jnp.float32
+    ) + jnp.einsum("td,tsc->dsc", in_x, gj_x, preferred_element_type=jnp.float32)
+    ip_o = back_project(gj_o)
+    grad_input = grad_first + ip_o + recv.astype(jnp.float32)
+
+    late = (grad_qkv_w.astype(jnp.bfloat16), grad_out_w.astype(jnp.bfloat16))
+    norm_parts = (grad_gain1, grad_bias1, grad_gain2, grad_bias2)
+    late, summed_up, summed_down, norm_parts = lax.optimization_barrier(
+        (late, summed_up, summed_down, norm_parts)
+    )
+    summed_qkv, summed_out = lax.psum(late, "dp")
+    summed_qkv, summed_out = summed_qkv.astype(jnp.float32), summed_out.astype(jnp.float32)
+    summed_gain1, summed_bias1, summed_gain2, summed_bias2 = lax.psum(norm_parts, ("dp", "tensor"))
+    return (
+        result.astype(jnp.bfloat16),
+        grad_input.astype(jnp.bfloat16),
+        summed_qkv,
+        summed_out,
+        summed_up,
+        summed_down,
+        summed_gain1,
+        summed_bias1,
+        summed_gain2,
+        summed_bias2,
+    )
+
+
 def solution(mesh):
     return jax.shard_map(
-        body,
+        body_pair if mesh.shape["tensor"] == 2 else body,
         mesh=mesh,
         in_specs=(
             P(("dp", "tensor"), None),

time: 581 us -> 488 us (0.84)
  waiting for transfers between devices: 286 us -> 224 us
  local copies, waits for them, and re-layouts: 72.9 us -> 25 us
  matrix products: 94.9 us -> 128 us
  other arithmetic: 51.4 us -> 35 us
    psum x2, waiting for transfers between devices: 131 us -> 99.4 us  [the longest x1 59.1 us: body_pair(): lax.psum((grad_up.astype(jnp.bfloat16), grad_down.astype(jnp.bfloat16)),...]
    ppermute x8, waiting for transfers between devices: 155 us -> 124 us  [_pair_swap(): return lax.ppermute(values, 'tensor', [(0, 1), (1, 0)])]
    dot_general x16 -> x22, matrix products: 54.4 us -> 80.1 us  [the longest x2 11.8 us: attend_row_back(): jnp.einsum('qhd,khd->hqk', grad_block, values, preferred_element_type=jnp...]
    dynamic_update_slice x8 -> x0, local copies, waits for them, and re-layouts: 18.5 us -> none  [the longest x4 10.6 us: body(): lax.map(attend_back, (joined_blocks, segment_blocks, log_totals, grad_mix...]
    reduce_sum x6 -> x3, other arithmetic: 16.6 us -> 3.39 us  [the longest x2 2.4 us: attend_row(): total = jnp.sum(expo, axis=-1, keepdims=True)]
    reshape x3 -> x0, local copies, waits for them, and re-layouts: 13 us -> none  [the longest x1 8.88 us: body(): joined.reshape(blocks, row_length, 3, local_heads, head_width)]
    another operation x0 -> x6, local copies, waits for them, and re-layouts: none -> 12.4 us  [attend_row_back(): stacked = jnp.stack([grad_query, grad_key, grad_value], axis=1)]
    while x6 -> x0, local copies, waits for them, and re-layouts: 10.9 us -> none  [the longest x1 7.61 us: body(): attended, log_totals = lax.map(attend, (joined_blocks, segment_blocks))]
  transfers between devices with their start and end apart: 10 -> 10, of which waited for: 10 -> 9; matrix products, arithmetic and copies ran while one was open for 17% -> 27% of each run, Pallas kernels for 0% -> 0%
where the time goes in v3:
time: 488 us; the launch traced here: 478 us
  waiting for transfers between devices  224 us (46%)
  matrix products  128 us (26%)
  blocking collectives  40.2 us (8%)
  other arithmetic  35 us (7%)
  local copies, waits for them, and re-layouts  25 us (5%)
  between operations  15.1 us (3%)
  starting transfers between devices  11.2 us (2%)
    ppermute x8, waiting for transfers between devices, _pair_swap(): return lax.ppermute(values, 'tensor', [(0, 1), (1, 0)])  124 us
    psum x1, waiting for transfers between devices, body_pair(): lax.psum((grad_up.astype(jnp.bfloat16), grad_down.astype(jnp.bfloat16)),...  59.1 us
    psum x1, waiting for transfers between devices, body_pair(): summed_qkv, summed_out = lax.psum(late, 'dp')  40.3 us
    psum x1, blocking collectives, body_pair(): lax.psum(norm_parts, ('dp', 'tensor'))  40.2 us
    dot_general x6, matrix products, contract_cols(): lax.dot_general(left, right, (((1,), (1,)), ((), ())), preferred_element_...  25.4 us
    dot_general x6, matrix products, contract_rows(): lax.dot_general(left, right, (((0,), (0,)), ((), ())), preferred_element_...  19.2 us
    another operation x6, local copies, waits for them, and re-layouts, attend_row_back(): stacked = jnp.stack([grad_query, grad_key, grad_value], axis=1)  12.4 us
    convert_element_type x2, other arithmetic, attend_row_back(): grad_scores = grad_scores.astype(jnp.bfloat16)  11.9 us
  transfers between devices with their start and end apart: 10, of which 9 were waited for; matrix products, arithmetic and copies ran while one was open for 27% of the time, Pallas kernels for 0%

profile of v3, /device:TPU:0, one launch (start us, length us, event | category | flops | bytes accessed | tf_op | source)
XLA Modules:
  0.0 478.1 jit_solution(11985224529656024085)
XLA Ops:
  7.2 3.0 collective-permute-start
  11.3 3.1 convolution_convert_fusion.1
  17.4 16.3 %collective-permute-done = bf16[512,1024]{1,0:T(8,128)(2,1)} collective-permute-done((bf16[512,1024]{1,0:T(8,128)(2,1)}, bf16[512,1024]{1,0:T(8,128)(2,1)}, u32[]{:S(2)}, u32[]{:S(2)}) %collective-permute-start) | collective-permute-done | bytes 1048608 | tf_op jit(solution)/shard_map/ppermute | solution.py:63
  33.7 3.1 convolution_convert_fusion
  39.6 2.2 copy-done.1
  47.7 20.8 %collective-permute-done.1 = bf16[512,1024]{1,0:T(8,128)(2,1)S(1)} collective-permute-done((bf16[512,1024]{1,0:T(8,128)(2,1)S(1)}, bf16[512,1024]{1,0:T(8,128)(2,1)S(1)}, u32[]{:S(2)}, u32[]{:S(2)}) %collective-permute-start.1) | collective-permute-done | bytes 1048608 | tf_op jit(solution)/shard_map/ppermute | solution.py:63
  71.8 22.0 %collective-permute-done.2 = bf16[512,1024]{1,0:T(8,128)(2,1)S(1)} collective-permute-done((bf16[512,1024]{1,0:T(8,128)(2,1)S(1)}, bf16[512,1024]{1,0:T(8,128)(2,1)S(1)}, u32[]{:S(2)}, u32[]{:S(2)}) %collective-permute-start.2) | collective-permute-done | bytes 1048608 | tf_op jit(solution)/shard_map/ppermute | solution.py:63
  93.8 4.1 multiply_convert_fusion.2
  97.8 2.3 convolution_convert_fusion.4
  101.5 2.9 multiply_convert_fusion.3
  104.3 18.6 %collective-permute-done.3 = bf16[512,1024]{1,0:T(8,128)(2,1)S(1)} collective-permute-done((bf16[512,1024]{1,0:T(8,128)(2,1)S(1)}, bf16[512,1024]{1,0:T(8,128)(2,1)S(1)}, u32[]{:S(2)}, u32[]{:S(2)}) %collective-permute-start.3) | collective-permute-done | bytes 1048608 | tf_op jit(solution)/shard_map/ppermute | solution.py:63
  122.9 2.7 fusion.60
  129.7 4.0 fusion.9
  133.7 2.4 fusion.67
  136.1 2.4 fusion.66
  138.5 12.1 %collective-permute-done.4 = bf16[512,1024]{1,0:T(8,128)(2,1)S(1)} collective-permute-done((bf16[512,1024]{1,0:T(8,128)(2,1)S(1)}, bf16[512,1024]{1,0:T(8,128)(2,1)S(1)}, u32[]{:S(2)}, u32[]{:S(2)}) %collective-permute-start.4) | collective-permute-done | bytes 1048608 | tf_op jit(solution)/shard_map/ppermute | solution.py:63
  150.6 5.3 %fusion.15 = bf16[512,2048]{1,0:T(8,128)(2,1)S(1)} fusion(f32[512,2048]{1,0:T(8,128)} %get-tuple-element.69, bf16[512,1024]{1,0:T(8,128)(2,1)S(1)} %collective-permute-done.4, bf16[2048,1024]{1,0:T(8,128)(2,1)S(1)} %copy-done.31), kind=kOutput, calls=%fused_computation.32 | convolution fusion | flops 2157969408 | bytes 11534336 | tf_op jit(solution)/shard_map/dot_general | solution.py:57
  155.9 3.4 convolution_convert_fusion.3
  159.8 4.6 add_convert_fusion.1
  164.4 4.6 add_convert_fusion
  169.3 11.2 %collective-permute-done.5 = bf16[512,1024]{1,0:T(8,128)(2,1)} collective-permute-done((bf16[512,1024]{1,0:T(8,128)(2,1)}, bf16[512,1024]{1,0:T(8,128)(2,1)}, u32[]{:S(2)}, u32[]{:S(2)}) %collective-permute-start.5) | collective-permute-done | bytes 1048608 | tf_op jit(solution)/shard_map/ppermute | solution.py:63
  180.5 8.3 %multiply_reduce_fusion.2 = (f32[1024]{0:T(1024)S(1)}, f32[512]{0:T(512)S(1)}, f32[512]{0:T(512)S(1)}, f32[1024]{0:T(1024)S(1)}, f32[512,1024]{1,0:T(8,128)S(1)}) fusion(f32[512,1024]{1,0:T(8,128)} %copy-done.5, f32[512]{0:T(512)S(1)} %add_rsqrt_fusion.1, f32[512]{0:T(512)S(1)} %broadcast_multiply_fusion.5, f32[1024]{0:T(1024)S(1)} %copy-done.28, ...), kind=kOutput, calls=%fused_computation.58 | convolution fusion | flops 2157966336 | bytes 14712832 | tf_op jit(solution)/shard_map/dot_general | solution.py:57
  188.8 2.3 fusion.59
  191.1 2.5 convolution_convert_fusion.6
  193.9 5.7 %fusion.37 = bf16[8,64,512]{2,1,0:T(8,128)(2,1)} fusion(bf16[512,8,64]{0,2,1:T(8,128)(2,1)S(1)} %bitcast.144, f32[8,512,512]{1,2,0:T(8,128)} %copy-done.2, f32[8,512]{1,0:T(8,128)S(1)} %log_add_fusion.1), kind=kOutput, calls=%fused_computation.86 | convolution fusion | flops 272891904 | bytes 9453568 | tf_op jit(solution)/shard_map/hqk,qhd->khd/dot_general | solution.py:257
  199.7 6.1 %multiply_reduce_fusion.1 = (f32[8,512]{1,0:T(8,128)S(1)}, f32[8,512,512]{1,2,0:T(8,128)}) fusion(f32[8,512,512]{1,2,0:T(8,128)S(1)} %bitcast.133, f32[8,512]{1,0:T(8,128)S(1)} %log_add_fusion.1, bf16[512,8,64]{0,2,1:T(8,128)(2,1)S(1)} %bitcast.145, bf16[512,3,8,64]{0,3,2,1:T(8,128)(2,1)} %bitcast.141), kind=kOutput, calls=%fused_computation.6 | convolution fusion | flops 274722816 | bytes 17858560 | tf_op jit(solution)/shard_map/qhd,khd->hqk/dot_general | solution.py:248
  207.9 7.1 %multiply_convert_fusion.1 = bf16[8,512,512]{1,2,0:T(8,128)(2,1)S(1)} fusion(f32[8,512,512]{1,2,0:T(8,128)} %get-tuple-element.74, f32[8,512,512]{1,2,0:T(8,128)} %copy-done.2, f32[8,512]{1,0:T(8,128)S(1)} %get-tuple-element.73, f32[8,512]{1,0:T(8,128)S(1)} %log_add_fusion.1), kind=kLoop, calls=%fused_computation.5 | loop fusion | flops 8388608 | bytes 21004288 | tf_op jit(solution)/shard_map/convert_element_type | solution.py:250
  217.0 2.6 fusion.43
  221.7 4.6 fusion.44
  228.4 6.4 %fusion.49 = f32[3,512,1024]{2,1,0:T(8,128)} fusion(bf16[512,1024]{1,0:T(8,128)(2,1)} %param.11, bf16[512,1,512]{2,0,1:T(8,128)(2,1)} %copy.30, bf16[512,1,512]{2,0,1:T(8,128)(2,1)} %copy.29, bf16[512,1,512]{2,0,1:T(8,128)(2,1)} %copy.28), kind=kOutput, calls=%fused_computation.96 | convolution fusion | flops 1612185600 | bytes 8912896 | tf_op jit(solution)/shard_map/td,tsc->dsc/dot_general | solution.py:350
  236.7 5.8 %fusion.40 = bf16[8,64,512]{2,1,0:T(8,128)(2,1)} fusion(bf16[512,8,64]{0,2,1:T(8,128)(2,1)S(1)} %bitcast.146, f32[8,512,512]{1,2,0:T(8,128)} %copy-done.1, f32[8,512]{1,0:T(8,128)S(1)} %log_add_fusion), kind=kOutput, calls=%fused_computation.87 | convolution fusion | flops 272891904 | bytes 9453568 | tf_op jit(solution)/shard_map/hqk,qhd->khd/dot_general | solution.py:257
  244.6 5.7 %multiply_reduce_fusion = (f32[8,512]{1,0:T(8,128)S(1)}, f32[8,512,512]{1,2,0:T(8,128)S(1)}) fusion(f32[8,512,512]{1,2,0:T(8,128)} %copy-done.1, f32[8,512]{1,0:T(8,128)S(1)} %log_add_fusion, bf16[512,8,64]{0,2,1:T(8,128)(2,1)} %bitcast.147, bf16[512,3,8,64]{0,3,2,1:T(8,128)(2,1)} %bitcast.136), kind=kOutput, calls=%fused_computation.3 | convolution fusion | flops 274722816 | bytes 17858560 | tf_op jit(solution)/shard_map/qhd,khd->hqk/dot_general | solution.py:248
  250.3 4.8 %multiply_convert_fusion = bf16[8,512,512]{1,2,0:T(8,128)(2,1)S(1)} fusion(f32[8,512,512]{1,2,0:T(8,128)S(1)} %get-tuple-element.72, f32[8,512,512]{1,2,0:T(8,128)} %copy-done.1, f32[8,512]{1,0:T(8,128)S(1)} %get-tuple-element.71, f32[8,512]{1,0:T(8,128)S(1)} %log_add_fusion), kind=kLoop, calls=%fused_computation.2 | loop fusion | flops 8388608 | bytes 21004288 | tf_op jit(solution)/shard_map/convert_element_type | solution.py:250
  257.1 2.6 fusion.45
  261.8 4.7 fusion.46
  268.6 2.1 fusion.65
  270.8 3.1 add_convert_fusion.3
  273.9 6.6 %fusion.24 = bf16[1024,3,512]{0,2,1:T(8,128)(2,1)} fusion(f32[3,512,1024]{2,1,0:T(8,128)} %fusion.49, bf16[512,1024]{1,0:T(8,128)(2,1)} %collective-permute-done, bf16[512,1,512]{2,0,1:T(8,128)(2,1)S(1)} %copy-done.13, bf16[512,1,512]{2,0,1:T(8,128)(2,1)S(1)} %copy-done.15, bf16[512,1,512]{2,0,1:T(8,128)(2,1)S(1)} %copy-done.14), kind=kOutput, calls=%fused_computation.43 | convolution fusion | flops 1615331328 | bytes 12058624 | tf_op jit(solution)/shard_map/td,tsc->dsc/dot_general | solution.py:352
  280.6 59.1 %all-reduce.8.cloned.1.call-done = (bf16[1024,2048]{1,0:T(8,128)(2,1)}, bf16[2048,1024]{1,0:T(8,128)(2,1)}) async-done(((bf16[1024,2048]{1,0:T(8,128)(2,1)}, bf16[2048,1024]{1,0:T(8,128)(2,1)}), (bf16[1024,2048]{1,0:T(8,128)(2,1)}, bf16[2048,1024]{1,0:T(8,128)(2,1)})) %all-reduce.8.cloned.1.call-update) | async-done | bytes 8388624 | tf_op jit(solution)/shard_map/psum | solution.py:326
  339.6 6.8 %convert_element_type.173 = f32[1024,2048]{1,0:T(8,128)} convert(bf16[1024,2048]{1,0:T(8,128)(2,1)} %get-tuple-element.50) | non-fusion elementwise | flops 2097152 | bytes 12582912 | tf_op jit(solution)/shard_map/convert_element_type | solution.py:329
  346.5 4.4 convert_element_type.175
  351.0 3.3 bitcast_convert_fusion
  355.8 23.4 %collective-permute-done.7 = bf16[512,1024]{1,0:T(8,128)(2,1)S(1)} collective-permute-done((bf16[512,1024]{1,0:T(8,128)(2,1)S(1)}, bf16[512,1024]{1,0:T(8,128)(2,1)S(1)}, u32[]{:S(2)}, u32[]{:S(2)}) %collective-permute-start.7) | collective-permute-done | bytes 1048608 | tf_op jit(solution)/shard_map/ppermute | solution.py:63
  379.3 2.8 fusion.33
  382.1 40.2 %all-reduce = (f32[1024]{0:T(1024)}, f32[1024]{0:T(1024)}, f32[1024]{0:T(1024)}, f32[1024]{0:T(1024)}) all-reduce(f32[1024]{0:T(1024)S(1)} %get-tuple-element.22, f32[1024]{0:T(1024)S(1)} %get-tuple-element.23, f32[1024]{0:T(1024)S(1)} %get-tuple-element.24, ...), channel_id=1, replica_groups=mesh['dp'=16,'tensor'=2] {'dp','tensor'}, use_global_device_ids=true, to_apply=%region_22.23 | all-reduce | flops 4096 | bytes 32768 | tf_op jit(solution)/shard_map/psum | solution.py:363
  422.2 40.3 %all-reduce.6.cloned.1.call-done = (bf16[1024,3,512]{0,2,1:T(8,128)(2,1)}, bf16[512,1024]{1,0:T(8,128)(2,1)}) async-done(((bf16[1024,3,512]{0,2,1:T(8,128)(2,1)}, bf16[512,1024]{1,0:T(8,128)(2,1)}), (bf16[1024,3,512]{0,2,1:T(8,128)(2,1)}, bf16[512,1024]{1,0:T(8,128)(2,1)})) %all-reduce.6.cloned.1.call-update) | async-done | bytes 4194320 | tf_op jit(solution)/shard_map/psum | solution.py:361
  462.6 2.8 convert_element_type.177
  465.4 5.4 %copy.39 = f32[1024,3,512]{2,0,1:T(8,128)} copy(bf16[1024,3,512]{0,2,1:T(8,128)(2,1)} %get-tuple-element.48) | data formatting | bytes 9437184
  (116 shorter events, 42.4 us)
Async XLA Ops:
  7.2 4.2 copy-start
  7.2 332.5 %all-reduce.8.cloned.1.call-start = ((), (), s32[]{:S(2)}) async-start(), calls=%async_computation.1 | async-start | bytes 16777216 | tf_op jit(solution)/shard_map/psum | solution.py:326
  7.2 26.5 %collective-permute-start = (bf16[512,1024]{1,0:T(8,128)(2,1)}, bf16[512,1024]{1,0:T(8,128)(2,1)}, u32[]{:S(2)}, u32[]{:S(2)}) collective-permute-start(bf16[512,1024]{1,0:T(8,128)(2,1)} %param.11), channel_id=1, source_target_pairs={{0,1},{1,0},{2,3},{3,2},{4,5},{5,4},{6,7},{7,6},{8,9},{9,8},{10,11... | collective-permute-start | bytes 3145736 | tf_op jit(solution)/shard_map/ppermute | solution.py:63
  14.4 31.5 %copy-start.9 = (bf16[512,3,512]{0,2,1:T(8,128)(2,1)}, bf16[512,3,512]{0,2,1:T(8,128)(2,1)S(1)}, u32[]{:S(2)}) copy-start(bf16[512,3,512]{0,2,1:T(8,128)(2,1)S(1)} %convolution_convert_fusion.1) | copy-start | bytes 4718596
  16.2 29.7 %copy-start.2 = (f32[8,512,512]{1,2,0:T(8,128)}, f32[8,512,512]{1,2,0:T(8,128)S(1)}, u32[]{:S(2)}) copy-start(f32[8,512,512]{1,2,0:T(8,128)S(1)} %get-tuple-element.63) | copy-start | bytes 25165828
  36.8 2.8 copy-start.8
  38.4 3.4 copy-start.1
  41.8 1.6 copy-start.20
  43.3 0.8 copy-start.23
  44.1 24.4 %copy-start.19 = (bf16[512,1024]{1,0:T(8,128)(2,1)S(1)}, bf16[512,1024]{1,0:T(8,128)(2,1)}, u32[]{:S(2)}) copy-start(bf16[512,1024]{1,0:T(8,128)(2,1)} %param.11) | copy-start | bytes 3145732
  44.1 24.4 %collective-permute-start.1 = (bf16[512,1024]{1,0:T(8,128)(2,1)S(1)}, bf16[512,1024]{1,0:T(8,128)(2,1)S(1)}, u32[]{:S(2)}, u32[]{:S(2)}) collective-permute-start(bf16[512,1024]{1,0:T(8,128)(2,1)S(1)} %convolution_convert_fusion.2), channel_id=1, source_target_pairs={{0,1},{1,0},{2,3},{3,2},{4,5},{5,4},{6,7},{7,6},{8,9},{9,8},{10,11... | collective-permute-start | bytes 3145736 | tf_op jit(solution)/shard_map/ppermute | solution.py:63
  47.7 22.1 %copy-start.17 = (bf16[8,64,512]{2,1,0:T(8,128)(2,1)}, bf16[8,64,512]{2,1,0:T(8,128)(2,1)S(1)}, u32[]{:S(2)}) copy-start(bf16[8,64,512]{2,1,0:T(8,128)(2,1)S(1)} %fusion.36) | copy-start | bytes 1572868
  68.5 1.3 copy-start.28
  68.5 1.3 copy-start.29
  69.4 53.5 %copy-start.5 = (f32[512,1024]{1,0:T(8,128)}, f32[512,1024]{1,0:T(8,128)S(1)}, u32[]{:S(2)}) copy-start(f32[512,1024]{1,0:T(8,128)S(1)} %get-tuple-element.57) | copy-start | bytes 6291460
  69.4 24.4 %copy-start.32 = (bf16[1024,2048]{1,0:T(8,128)(2,1)S(1)}, bf16[1024,2048]{1,0:T(8,128)(2,1)}, u32[]{:S(2)}) copy-start(bf16[1024,2048]{1,0:T(8,128)(2,1)} %param.15) | copy-start | bytes 12582916
  70.2 27.6 %copy-start.31 = (bf16[2048,1024]{1,0:T(8,128)(2,1)S(1)}, bf16[2048,1024]{1,0:T(8,128)(2,1)}, u32[]{:S(2)}) copy-start(bf16[2048,1024]{1,0:T(8,128)(2,1)} %param.16) | copy-start | bytes 12582916
  70.2 23.5 %collective-permute-start.2 = (bf16[512,1024]{1,0:T(8,128)(2,1)S(1)}, bf16[512,1024]{1,0:T(8,128)(2,1)S(1)}, u32[]{:S(2)}, u32[]{:S(2)}) collective-permute-start(bf16[512,1024]{1,0:T(8,128)(2,1)S(1)} %fusion.34), channel_id=1, source_target_pairs={{0,1},{1,0},{2,3},{3,2},{4,5},{5,4},{6,7},{7,6},{8,9},{9,8},{10,11... | collective-permute-start | bytes 3145736 | tf_op jit(solution)/shard_map/ppermute | solution.py:63
  100.2 22.7 %collective-permute-start.3 = (bf16[512,1024]{1,0:T(8,128)(2,1)S(1)}, bf16[512,1024]{1,0:T(8,128)(2,1)S(1)}, u32[]{:S(2)}, u32[]{:S(2)}) collective-permute-start(bf16[512,1024]{1,0:T(8,128)(2,1)S(1)} %convolution_convert_fusion.4), channel_id=1, source_target_pairs={{0,1},{1,0},{2,3},{3,2},{4,5},{5,4},{6,7},{7,6},{8,9},{9,8},{10,11... | collective-permute-start | bytes 3145736 | tf_op jit(solution)/shard_map/ppermute | solution.py:63
  122.9 3.1 copy-start.11
  122.9 3.1 copy-start.27
  125.6 3.2 copy-start.7
  125.6 1.4 copy-start.30
  128.8 21.8 %collective-permute-start.4 = (bf16[512,1024]{1,0:T(8,128)(2,1)S(1)}, bf16[512,1024]{1,0:T(8,128)(2,1)S(1)}, u32[]{:S(2)}, u32[]{:S(2)}) collective-permute-start(bf16[512,1024]{1,0:T(8,128)(2,1)S(1)} %get-tuple-element.58), channel_id=1, source_target_pairs={{0,1},{1,0},{2,3},{3,2},{4,5},{5,4},{6,7},{7,6},{8,9},{9,8},{10,11... | collective-permute-start | bytes 3145736 | tf_op jit(solution)/shard_map/ppermute | solution.py:63
  133.6 2.4 copy-start.33
  159.2 21.2 %collective-permute-start.5 = (bf16[512,1024]{1,0:T(8,128)(2,1)}, bf16[512,1024]{1,0:T(8,128)(2,1)}, u32[]{:S(2)}, u32[]{:S(2)}) collective-permute-start(bf16[512,1024]{1,0:T(8,128)(2,1)} %convolution_convert_fusion.3), channel_id=1, source_target_pairs={{0,1},{1,0},{2,3},{3,2},{4,5},{5,4},{6,7},{7,6},{8,9},{9,8},{10,11... | collective-permute-start | bytes 3145736 | tf_op jit(solution)/shard_map/ppermute | solution.py:63
  169.0 293.6 %all-reduce.6.cloned.1.call-start = ((), (), s32[]{:S(2)}) async-start(), calls=%async_computation | async-start | bytes 8388608 | tf_op jit(solution)/shard_map/psum | solution.py:361
  169.3 19.5 %copy-start.6 = (f32[512,1024]{1,0:T(8,128)S(1)}, f32[512,1024]{1,0:T(8,128)}, u32[]{:S(2)}) copy-start(f32[512,1024]{1,0:T(8,128)} %copy-done.5) | copy-start | bytes 6291460
  188.8 2.3 copy-start.21
  188.8 10.9 %slice-start = ((s8[8388608]{0:T(1024)(128)(4,1)}), s8[4194304]{0:T(1024)(128)(4,1)S(1)}, s32[]{:S(2)}) async-start(s8[8388608]{0:T(1024)(128)(4,1)} %bitcast.132), calls=%async_computation.2 | async-start | bytes 8388608
  191.1 8.6 %slice-start.1 = ((s8[8388608]{0:T(1024)(128)(4,1)}), s8[4194304]{0:T(1024)(128)(4,1)S(1)}, s32[]{:S(2)}) async-start(s8[8388608]{0:T(1024)(128)(4,1)} %bitcast.132), calls=%async_computation.3 | async-start | bytes 8388608
  193.6 41.1 %collective-permute-start.6 = (bf16[512,1024]{1,0:T(8,128)(2,1)}, bf16[512,1024]{1,0:T(8,128)(2,1)}, u32[]{:S(2)}, u32[]{:S(2)}) collective-permute-start(bf16[512,1024]{1,0:T(8,128)(2,1)} %get-tuple-element.52), channel_id=1, source_target_pairs={{0,1},{1,0},{2,3},{3,2},{4,5},{5,4},{6,7},{7,6},{8,9},{9,8},{10,11... | collective-permute-start | bytes 3145736 | tf_op jit(solution)/shard_map/ppermute | solution.py:63
  215.0 2.0 copy-start.3
  228.4 6.4 %copy-start.22 = (bf16[512,1024]{1,0:T(8,128)(2,1)S(1)}, bf16[512,1024]{1,0:T(8,128)(2,1)}, u32[]{:S(2)}) copy-start(bf16[512,1024]{1,0:T(8,128)(2,1)} %param.14) | copy-start | bytes 3145732
  236.7 5.8 %copy-start.12 = (bf16[512,512]{0,1:T(8,128)(2,1)}, bf16[512,512]{0,1:T(8,128)(2,1)S(1)}, u32[]{:S(2)}) copy-start(bf16[512,512]{0,1:T(8,128)(2,1)S(1)} %convolution_convert_fusion.5) | copy-start | bytes 1572868
  255.1 2.0 copy-start.4
  268.6 2.2 copy-start.18
  270.8 3.1 copy-start.13
  270.8 3.1 copy-start.14
  270.8 3.1 copy-start.15
  339.6 6.8 %copy-start.10 = (bf16[2048,1024]{1,0:T(8,128)(2,1)S(1)}, bf16[2048,1024]{1,0:T(8,128)(2,1)}, u32[]{:S(2)}) copy-start(bf16[2048,1024]{1,0:T(8,128)(2,1)} %get-tuple-element.51) | copy-start | bytes 12582916
  350.9 28.3 %copy-start.16 = (f32[512,1024]{1,0:T(8,128)S(1)}, f32[512,1024]{1,0:T(8,128)}, u32[]{:S(2)}) copy-start(f32[512,1024]{1,0:T(8,128)} %get-tuple-element.53) | copy-start | bytes 6291460
  350.9 28.3 %copy-start.24 = (bf16[512,1,512]{2,0,1:T(8,128)(2,1)S(1)}, bf16[512,1,512]{2,0,1:T(8,128)(2,1)}, u32[]{:S(2)}) copy-start(bf16[512,1,512]{2,0,1:T(8,128)(2,1)} %copy.30) | copy-start | bytes 1572868
  350.9 28.3 %copy-start.25 = (bf16[512,1,512]{2,0,1:T(8,128)(2,1)S(1)}, bf16[512,1,512]{2,0,1:T(8,128)(2,1)}, u32[]{:S(2)}) copy-start(bf16[512,1,512]{2,0,1:T(8,128)(2,1)} %copy.28) | copy-start | bytes 1572868
  350.9 28.3 %copy-start.26 = (bf16[512,1,512]{2,0,1:T(8,128)(2,1)S(1)}, bf16[512,1,512]{2,0,1:T(8,128)(2,1)}, u32[]{:S(2)}) copy-start(bf16[512,1,512]{2,0,1:T(8,128)(2,1)} %copy.29) | copy-start | bytes 1572868
  354.3 24.9 %collective-permute-start.7 = (bf16[512,1024]{1,0:T(8,128)(2,1)S(1)}, bf16[512,1024]{1,0:T(8,128)(2,1)S(1)}, u32[]{:S(2)}, u32[]{:S(2)}) collective-permute-start(bf16[512,1024]{1,0:T(8,128)(2,1)S(1)} %bitcast_convert_fusion), channel_id=1, source_target_pairs={{0,1},{1,0},{2,3},{3,2},{4,5},{5,4},{6,7},{7,6},{8,9},{9,8},{10,11... | collective-permute-start | bytes 3145736 | tf_op jit(solution)/shard_map/ppermute | solution.py:63
Sparse Core Ops, SparseCore 0:
  169.2 170.4 all-reduce.7
  351.0 111.5 all-reduce.5
